TPU v7x, 128 devices: a whole 4x4x4 slice. The times are simulated.
128 devices in a mesh: dp: 32 (over x, z, core), mp: 4 (over y).
Axes of the slice: x: 4, y: 4, z: 4, core: 2. Of those that a mesh axis runs over, the one named last changes fastest.
Arguments:
- query_rows: bfloat16 [2048, 2560], P('dp', 'mp'), may hold values from -48 to 48
- doc_rows: bfloat16 [2048, 2560], P('dp', 'mp'), may hold values from -48 to 48
- head: bfloat16 [2560, 2560], P(None, 'mp'), may hold values from -0.125 to 0.125
- logit_scale: float32 [7], replicated, may hold values from 1 to 3
- loss_grad: float32 [2048, 7], P('dp'), may hold values from 0.5 to 2
- shortlist: int32 [2048, 128], P('dp'), may hold values from 0 to 127, as said below
- send_rows: int32 [32, 128], P('dp'), may hold values from -1 to 63, as said below
Outputs:
- query_grad: bfloat16 [2048, 2560], P('dp', 'mp')
- doc_grad: bfloat16 [2048, 2560], P('dp', 'mp')
- head_grad: float32 [2560, 2560], P('dp', 'mp')
Inputs may be any that keep to these rules, and one draw needn't show every extreme that they name: shortlist[i, n] is a slot o * 4 + j of the rows fetched for the owner of query i, and send_rows at place j of the block owner o sends to that owner is never -1. send_rows[o, r * 4 + j] is a row among owner o's 64 documents, sent to owner r at place j; in each block of 4 places the rows are distinct and come first, -1 fills the rest; the block an owner sends to itself is always full.
All inputs are finite; a program needn't handle non-finite values.
Results may differ from a plain program's by a relative error of at most 0.014.
The roundings to bfloat16 on the way count: a program that leaves them out, or rounds other values in their place, can miss the bound.
Values may be sent and summed in bfloat16 or wider, within the bound.
A program may use at most 64 MiB of HBM per device.

v0:
```python
import jax
import jax.numpy as jnp
from jax import lax
from jax.sharding import PartitionSpec as P

NW = 7


def in_one_piece(arrays, axis, dim, along):
    widths = [a.shape[along] for a in arrays]
    both = jnp.concatenate(arrays, axis=along)
    filled = lax.all_gather(both, axis, axis=dim, tiled=True)
    return tuple(jnp.split(filled, [sum(widths[:k]) for k in range(1, len(widths))], axis=along))


def from_everyone(x, axis):
    copies = jnp.broadcast_to(x, (lax.axis_size(axis), *x.shape))
    return lax.all_to_all(copies, axis, split_axis=0, concat_axis=0, tiled=True)


def of_everyone(x, axis):
    return from_everyone(x, axis).sum(axis=0)


def in_one(arrays, axis):
    ends = [0]
    for a in arrays:
        ends.append(ends[-1] + a.size)
    total = of_everyone(jnp.concatenate([a.ravel() for a in arrays]), axis)
    return tuple((total[b:e].reshape(a.shape) for a, b, e in zip(arrays, ends, ends[1:])))


def width_bounds(feature_total):
    return [0] + [feature_total // 2 ** (NW - 1 - width_level) for width_level in range(NW)]


def softmax_terms(neg_score, pos_score, width_scale, loss_weight):
    neg_logit = neg_score * width_scale[:, None, None]
    pos_logit = pos_score * width_scale[:, None]
    highest = jnp.maximum(jnp.max(neg_logit, axis=2), pos_logit)
    neg_exp = jnp.exp(neg_logit - highest[:, :, None])
    pos_exp = jnp.exp(pos_logit - highest)
    denominator = jnp.sum(neg_exp, axis=2) + pos_exp
    row_weight = loss_weight * width_scale[:, None]
    neg_grad = neg_exp * (row_weight / denominator)[:, :, None]
    pos_grad = row_weight * (pos_exp / denominator - 1.0)
    return (neg_grad, pos_grad)


def suffix_sum(values):
    return jnp.flip(jnp.cumsum(jnp.flip(values, 0), axis=0), 0)


def on_device(query_rows, doc_rows, head, logit_scale, loss_grad, shortlist, send_rows):
    queries = shortlist.shape[0]
    slice_cols = head.shape[1]
    feature_total = head.shape[0]
    fetch_total = send_rows.shape[1]
    bounds = width_bounds(feature_total)
    whole_query, whole_doc = in_one_piece((query_rows, doc_rows), "mp", 1, 0)
    query_proj = jnp.dot(whole_query, head, preferred_element_type=jnp.float32).astype(jnp.bfloat16)
    doc_proj = jnp.dot(whole_doc, head, preferred_element_type=jnp.float32).astype(jnp.bfloat16)
    col_ids = lax.axis_index("mp") * slice_cols + jnp.arange(slice_cols, dtype=jnp.int32)
    seg_float = jnp.stack(
        [
            ((col_ids >= bounds[segment]) & (col_ids < bounds[segment + 1])).astype(jnp.float32)
            for segment in range(NW)
        ]
    )
    prefix_mask = jnp.stack([col_ids < bounds[level + 1] for level in range(NW)]).astype(
        jnp.bfloat16
    )
    local_rows = send_rows[0]
    outgoing = jnp.take(doc_proj, jnp.maximum(local_rows, 0), axis=0)
    fetched = lax.all_to_all(outgoing, "dp", split_axis=0, concat_axis=0, tiled=True)
    slot_table = (
        shortlist[:, :, None] == jnp.arange(fetch_total, dtype=jnp.int32)[None, None, :]
    ).astype(jnp.float32)
    masked_query = query_proj[None, :, :] * prefix_mask[:, None, :]
    part_scores = jnp.einsum(
        "wqc,rc->wqr", masked_query, fetched, preferred_element_type=jnp.float32
    )
    part_neg = jnp.einsum("wqt,qnt->wqn", part_scores, slot_table, precision=lax.Precision.HIGHEST)
    pos_prod = query_proj.astype(jnp.float32) * doc_proj.astype(jnp.float32)
    part_pos = jnp.cumsum(
        jnp.einsum("sc,ic->si", seg_float, pos_prod, precision=lax.Precision.HIGHEST), axis=0
    )
    widths = jnp.array(bounds[1:], jnp.float32)
    width_scale = logit_scale / jnp.sqrt(widths)
    neg_score, pos_score = in_one((part_neg, part_pos), "mp")
    neg_grad, pos_grad = softmax_terms(neg_score, pos_score, width_scale, loss_grad.T)
    seg_neg = suffix_sum(neg_grad)
    seg_pos = suffix_sum(pos_grad)
    coeff_dense = jnp.einsum(
        "wqn,qnt->wqt", seg_neg, slot_table, precision=lax.Precision.HIGHEST
    ).astype(jnp.bfloat16)
    pos_cols = jnp.einsum("si,sc->ic", seg_pos, seg_float, precision=lax.Precision.HIGHEST)
    query_levels = jnp.einsum(
        "sir,rc->sic", coeff_dense, fetched, preferred_element_type=jnp.float32
    )
    query_back = jnp.sum(query_levels * seg_float[:, None, :], axis=0)
    grad_query = (query_back + pos_cols * doc_proj.astype(jnp.float32)).astype(jnp.bfloat16)
    fetched_levels = jnp.einsum(
        "sir,ic->src", coeff_dense, query_proj, preferred_element_type=jnp.float32
    )
    fetched_grad = jnp.sum(fetched_levels * seg_float[:, None, :], axis=0)
    returned = lax.all_to_all(fetched_grad, "dp", split_axis=0, concat_axis=0, tiled=True)
    targets = jnp.where(local_rows >= 0, local_rows, queries)
    doc_back = jnp.zeros((queries, slice_cols), jnp.float32).at[targets].add(returned, mode="drop")
    grad_doc = (pos_cols * query_proj.astype(jnp.float32) + doc_back).astype(jnp.bfloat16)
    contract = (((1,), (1,)), ((), ()))
    head_rows = lax.all_to_all(head, "mp", split_axis=0, concat_axis=1, tiled=True)
    full_query, full_doc = in_one_piece((grad_query, grad_doc), "mp", 1, 0)
    query_grad = lax.dot_general(
        full_query, head_rows, contract, preferred_element_type=jnp.float32
    ).astype(jnp.bfloat16)
    doc_grad = lax.dot_general(
        full_doc, head_rows, contract, preferred_element_type=jnp.float32
    ).astype(jnp.bfloat16)
    row_contract = (((0,), (0,)), ((), ()))
    query_term = lax.dot_general(
        whole_query, grad_query, row_contract, preferred_element_type=jnp.float32
    )
    doc_term = lax.dot_general(
        whole_doc, grad_doc, row_contract, preferred_element_type=jnp.float32
    )
    head_grad = lax.psum_scatter(
        (query_term + doc_term).astype(jnp.bfloat16), "dp", scatter_dimension=0, tiled=True
    ).astype(jnp.float32)
    return (query_grad, doc_grad, head_grad)


def solution(mesh):
    placed = (
        P("dp", "mp"),
        P("dp", "mp"),
        P(None, "mp"),
        P(),
        P("dp", None),
        P("dp", None),
        P("dp", None),
    )
    return jax.shard_map(
        on_device,
        mesh=mesh,
        in_specs=placed,
        out_specs=(P("dp", "mp"), P("dp", "mp"), P("dp", "mp")),
        check_vma=False,
    )
```

profile of v0, /device:TPU:1, one launch (start us, length us, event | category | flops | bytes accessed | tf_op | source)
XLA Modules:
  0.0 178.1 jit_solution(8546073559253771080)
XLA Ops:
  7.2 0.7 fusion.36
  7.8 0.7 compare_reduce_fusion
  8.5 0.9 pad_maximum_fusion.1
  9.4 13.2 %all_gather.6 = bf16[128,2560]{1,0:T(8,128)(2,1)S(1)} all-gather(bf16[128,640]{1,0:T(8,128)(2,1)S(1)} %pad_maximum_fusion.1), channel_id=1, replica_groups=mesh['dp'=32,'mp'=4] {'mp'}, dimensions={1}, use_global_device_ids=true | all-gather | bytes 819200 | tf_op jit(solution)/shard_map/all_gather | solution.py:12
  22.7 2.6 %convolution_convert_fusion.2 = bf16[64,640]{1,0:T(8,128)(2,1)S(1)} fusion(bf16[2560,640]{1,0:T(8,128)(2,1)} %param.10, bf16[128,2560]{1,0:T(8,128)(2,1)S(1)} %all_gather.6), kind=kOutput, calls=%fused_computation.16 | convolution fusion | flops 209756160 | bytes 3686400 | tf_op jit(solution)/shard_map/dot_general | solution.py:62
  25.3 0.9 gather_fusion
  26.2 0.1 le.17
  26.4 0.8 broadcast_select_fusion
  27.2 9.9 %all-to-all-start = ((bf16[32,4,640]{2,1,0:T(4,128)(2,1)}), bf16[32,4,640]{2,1,0:T(4,128)(2,1)S(1)}, u32[]{:S(2)}, u32[]{:S(2)}) async-start(bf16[32,4,640]{2,1,0:T(4,128)(2,1)} %broadcast_select_fusion), calls=%async_computation | async-start | bytes 327680 | tf_op jit(solution)/shard_map/all_to_all | solution.py:75
  37.2 2.6 %convolution_convert_fusion.3 = bf16[64,640]{1,0:T(8,128)(2,1)S(1)} fusion(bf16[2560,640]{1,0:T(8,128)(2,1)} %param.10, bf16[128,2560]{1,0:T(8,128)(2,1)S(1)} %all_gather.6), kind=kOutput, calls=%fused_computation.17 | convolution fusion | flops 209756160 | bytes 3686400 | tf_op jit(solution)/shard_map/dot_general | solution.py:61
  40.0 0.2 fusion.23
  40.2 0.1 reduce_window_sum.28
  40.3 0.1 reshape.270
  40.3 4.8 %all-to-all-done = bf16[32,4,640]{2,1,0:T(4,128)(2,1)S(1)} async-done(((bf16[32,4,640]{2,1,0:T(4,128)(2,1)}), bf16[32,4,640]{2,1,0:T(4,128)(2,1)S(1)}, u32[]{:S(2)}, u32[]{:S(2)}) %all-to-all-start) | async-done | bytes 163872 | tf_op jit(solution)/shard_map/all_to_all | solution.py:75
  45.2 0.3 fusion.8
  45.5 4.7 %fusion.5 = f32[7,64,128]{2,0,1:T(8,128)S(1)} fusion(s32[64,128]{1,0:T(8,128)S(1)} %copy-done.3, f32[7,64,128]{2,1,0:T(8,128)S(1)} %fusion.8), kind=kOutput, calls=%fused_computation.11 | convolution fusion | flops 89128960 | bytes 491520 | tf_op jit(solution)/shard_map/wqt,qnt->wqn/dot_general | solution.py:83
  50.2 0.1 copy.32
  50.3 1.4 broadcast_in_dim.15
  51.8 4.3 %all-to-all-start.1 = ((f32[4,1,57792]{2,1,0:T(1,128)}), f32[4,1,57792]{2,1,0:T(1,128)S(1)}, u32[]{:S(2)}, u32[]{:S(2)}) async-start(f32[4,1,57792]{2,1,0:T(1,128)} %broadcast_in_dim.15), calls=%async_computation.1 | async-start | bytes 1851392 | tf_op jit(solution)/shard_map/all_to_all | solution.py:18
  56.1 13.2 %all-to-all-done.1 = f32[4,1,57792]{2,1,0:T(1,128)S(1)} async-done(((f32[4,1,57792]{2,1,0:T(1,128)}), f32[4,1,57792]{2,1,0:T(1,128)S(1)}, u32[]{:S(2)}, u32[]{:S(2)}) %all-to-all-start.1) | async-done | bytes 924704 | tf_op jit(solution)/shard_map/all_to_all | solution.py:18
  69.3 0.9 reduce_sum.36
  70.3 0.1 reshape.272
  70.3 0.2 multiply_reduce_fusion.1
  70.5 0.1 multiply_maximum_fusion
  70.6 0.3 fusion.22
  70.9 0.1 bitcast_divide_fusion
  71.0 0.2 fusion.21
  71.2 0.3 fusion.38
  71.5 2.9 %fusion.7 = bf16[7,64,128]{2,0,1:T(8,128)(2,1)S(1)} fusion(s32[64,128]{1,0:T(8,128)S(1)} %copy-done.3, f32[7,64,128]{2,1,0:T(8,128)S(1)} %rev.15), kind=kOutput, calls=%fused_computation.13 | convolution fusion | flops 89186304 | bytes 376832 | tf_op jit(solution)/shard_map/wqn,qnt->wqt/dot_general | solution.py:94
  74.4 0.3 fusion.4
  74.7 0.5 multiply_reduce_fusion
  75.3 0.8 all_to_all.35
  76.1 5.0 %all-to-all-start.2 = ((f32[32,4,640]{2,1,0:T(4,128)}), f32[32,4,640]{2,1,0:T(4,128)S(1)}, u32[]{:S(2)}, u32[]{:S(2)}) async-start(f32[32,4,640]{2,1,0:T(4,128)} %all_to_all.35), calls=%async_computation.2 | async-start | bytes 655360 | tf_op jit(solution)/shard_map/all_to_all | solution.py:107
  81.1 0.0 reduce-scatter.2.cloned.1.call-start
  81.2 0.3 fusion.25
  81.5 3.8 %fusion.14 = f32[2560,640]{1,0:T(8,128)} fusion(bf16[64,640]{1,0:T(8,128)(2,1)S(1)} %get-tuple-element.3, bf16[128,2560]{1,0:T(8,128)(2,1)S(1)} %all_gather.6), kind=kOutput, calls=%fused_computation.24 | convolution fusion | flops 209715200 | bytes 6963200 | tf_op jit(solution)/shard_map/dot_general | solution.py:121
  85.3 5.6 %all-to-all-done.2 = f32[32,4,640]{2,1,0:T(4,128)S(1)} async-done(((f32[32,4,640]{2,1,0:T(4,128)}), f32[32,4,640]{2,1,0:T(4,128)S(1)}, u32[]{:S(2)}, u32[]{:S(2)}) %all-to-all-start.2) | async-done | bytes 327712 | tf_op jit(solution)/shard_map/all_to_all | solution.py:107
  90.9 0.1 reshape.285
  91.0 1.5 scatter_fusion
  92.5 5.7 %add_convert_fusion = bf16[2560,640]{1,0:T(8,128)(2,1)} fusion(f32[2560,640]{1,0:T(8,128)} %fusion.14, bf16[64,640]{1,0:T(8,128)(2,1)S(1)} %convert_element_type.110, bf16[128,2560]{1,0:T(8,128)(2,1)S(1)} %all_gather.6), kind=kOutput, calls=%fused_computation.2 | convolution fusion | flops 212992000 | bytes 10240000 | tf_op jit(solution)/shard_map/dot_general | solution.py:124
  98.2 3.7 %all-to-all-start.3 = ((bf16[4,640,640]{2,1,0:T(8,128)(2,1)}), bf16[4,640,640]{2,1,0:T(8,128)(2,1)S(1)}, u32[]{:S(2)}, u32[]{:S(2)}) async-start(bf16[4,640,640]{2,1,0:T(8,128)(2,1)} %bitcast.9), calls=%async_computation.3 | async-start | bytes 6553600 | tf_op jit(solution)/shard_map/all_to_all | solution.py:112
  102.0 46.8 %all_gather.7 = bf16[128,2560]{1,0:T(8,128)(2,1)} all-gather(bf16[128,640]{1,0:T(8,128)(2,1)S(1)} %pad_maximum_fusion.2), channel_id=1, replica_groups=mesh['dp'=32,'mp'=4] {'mp'}, dimensions={1}, use_global_device_ids=true | all-gather | bytes 819200 | tf_op jit(solution)/shard_map/all_gather | solution.py:12
  148.8 1.7 copy-done
  150.5 4.2 %copy.37 = bf16[640,4,640]{0,2,1:T(8,128)(2,1)S(1)} copy(bf16[640,4,640]{2,0,1:T(8,128)(2,1)} %bitcast.38) | data formatting | bytes 6553600 | tf_op jit(solution)/shard_map/all_to_all | solution.py:112
  154.7 2.4 %convolution_convert_fusion = bf16[64,640]{1,0:T(8,128)(2,1)} fusion(bf16[640,2560]{0,1:T(8,128)(2,1)S(1)} %bitcast.36, bf16[128,2560]{1,0:T(8,128)(2,1)} %all_gather.7), kind=kOutput, calls=%fused_computation.14 | convolution fusion | flops 209756160 | bytes 3686400 | tf_op jit(solution)/shard_map/dot_general | solution.py:117
  157.1 1.3 convolution_convert_fusion.1
  158.4 11.3 %reduce-scatter.2.cloned.1.call-done = bf16[80,640]{1,0:T(8,128)(2,1)} async-done(((bf16[2560,640]{1,0:T(8,128)(2,1)}), bf16[80,640]{1,0:T(8,128)(2,1)}) %reduce-scatter.2.cloned.1.call-update) | async-done | bytes 102416 | tf_op jit(solution)/shard_map/reduce_scatter | solution.py:127
  169.7 1.6 convert_element_type.114
  (39 shorter events, 0.5 us)
Async XLA Ops:
  26.2 19.3 %copy-start.3 = (s32[64,128]{1,0:T(8,128)S(1)}, s32[64,128]{1,0:T(8,128)}, u32[]{:S(2)}) copy-start(s32[64,128]{1,0:T(8,128)} %param.13) | copy-start | bytes 98308
  27.2 17.9 %all-to-all-start = ((bf16[32,4,640]{2,1,0:T(4,128)(2,1)}), bf16[32,4,640]{2,1,0:T(4,128)(2,1)S(1)}, u32[]{:S(2)}, u32[]{:S(2)}) async-start(bf16[32,4,640]{2,1,0:T(4,128)(2,1)} %broadcast_select_fusion), calls=%async_computation | async-start | bytes 327680 | tf_op jit(solution)/shard_map/all_to_all | solution.py:75
  45.1 11.0 %copy-start.4 = (f32[7]{0:T(128)S(1)}, f32[7]{0:T(128)}, u32[]{:S(2)}) copy-start(f32[7]{0:T(128)} %param.11) | copy-start | bytes 88
  45.1 11.0 %copy-start.5 = (f32[7]{0:T(128)S(1)}, f32[7]{0:T(128)}, u32[]{:S(2)}) copy-start(f32[7]{0:T(128)} %constant.60) | copy-start | bytes 88
  50.2 20.6 %copy-start.2 = (f32[64,7]{0,1:T(8,128)S(1)}, f32[64,7]{0,1:T(8,128)}, u32[]{:S(2)}) copy-start(f32[64,7]{0,1:T(8,128)} %param.12) | copy-start | bytes 5380
  51.8 17.6 %all-to-all-start.1 = ((f32[4,1,57792]{2,1,0:T(1,128)}), f32[4,1,57792]{2,1,0:T(1,128)S(1)}, u32[]{:S(2)}, u32[]{:S(2)}) async-start(f32[4,1,57792]{2,1,0:T(1,128)} %broadcast_in_dim.15), calls=%async_computation.1 | async-start | bytes 1851392 | tf_op jit(solution)/shard_map/all_to_all | solution.py:18
  76.1 14.8 %all-to-all-start.2 = ((f32[32,4,640]{2,1,0:T(4,128)}), f32[32,4,640]{2,1,0:T(4,128)S(1)}, u32[]{:S(2)}, u32[]{:S(2)}) async-start(f32[32,4,640]{2,1,0:T(4,128)} %all_to_all.35), calls=%async_computation.2 | async-start | bytes 655360 | tf_op jit(solution)/shard_map/all_to_all | solution.py:107
  81.1 88.6 %reduce-scatter.2.cloned.1.call-start = ((), (), s32[]{:S(2)}) async-start(), calls=%async_computation.5 | async-start | bytes 3379200 | tf_op jit(solution)/shard_map/reduce_scatter | solution.py:127
  98.2 50.6 %all-to-all-start.3 = ((bf16[4,640,640]{2,1,0:T(8,128)(2,1)}), bf16[4,640,640]{2,1,0:T(8,128)(2,1)S(1)}, u32[]{:S(2)}, u32[]{:S(2)}) async-start(bf16[4,640,640]{2,1,0:T(8,128)(2,1)} %bitcast.9), calls=%async_computation.3 | async-start | bytes 6553600 | tf_op jit(solution)/shard_map/all_to_all | solution.py:112
  148.8 1.7 copy-start
  154.7 2.4 %copy-start.1 = (bf16[128,2560]{1,0:T(8,128)(2,1)S(1)}, bf16[128,2560]{1,0:T(8,128)(2,1)}, u32[]{:S(2)}) copy-start(bf16[128,2560]{1,0:T(8,128)(2,1)} %all_gather.7) | copy-start | bytes 1966084
Sparse Core Ops, SparseCore 0:
  98.3 71.3 reduce-scatter.1
where the time goes:
time: 180 us; the launch traced here: 178 us
  blocking collectives  60.1 us (33%)
  waiting for transfers between devices  34.9 us (19%)
  matrix products  27.6 us (15%)
  starting transfers between devices  23 us (13%)
  between operations  14.4 us (8%)
  local copies, waits for them, and re-layouts  9.72 us (5%)
  other arithmetic  8.45 us (5%)
    all_gather x2, blocking collectives, in_one_piece(): filled = lax.all_gather(both, axis, axis=dim, tiled=True)  60.1 us
    all_to_all x1, waiting for transfers between devices, from_everyone(): return lax.all_to_all(copies, axis, split_axis=0, concat_axis=0, tiled=True)  13.2 us
    reduce_scatter x1, waiting for transfers between devices, on_device(): lax.psum_scatter((query_term + doc_term).astype(jnp.bfloat16), 'dp', scat...  11.3 us
    all_to_all x1, starting transfers between devices, on_device(): lax.all_to_all(outgoing, 'dp', split_axis=0, concat_axis=0, tiled=True)  9.93 us
    dot_general x1, matrix products, on_device(): lax.dot_general(whole_doc, grad_doc, row_contract, preferred_element_type...  5.67 us
    all_to_all x1, waiting for transfers between devices, on_device(): lax.all_to_all(fetched_grad, 'dp', split_axis=0, concat_axis=0, tiled=True)  5.6 us
    all_to_all x1, starting transfers between devices, on_device(): lax.all_to_all(fetched_grad, 'dp', split_axis=0, concat_axis=0, tiled=True)  5.02 us
    all_to_all x1, waiting for transfers between devices, on_device(): lax.all_to_all(outgoing, 'dp', split_axis=0, concat_axis=0, tiled=True)  4.76 us
  transfers between devices with their start and end apart: 5, of which 4 were waited for; matrix products, arithmetic and copies ran while one was open for 8% of the time, Pallas kernels for 0%

commit v1 on v0

v1 whole, which is shorter than its diff:
```python
import functools
import math

import jax
import jax.numpy as jnp
from jax import lax
from jax.experimental import pallas as pl
from jax.experimental.pallas import tpu as pltpu
from jax.sharding import PartitionSpec as P

NW = 7
LOCAL = 5
MESH = pl.DeviceIdType.MESH
F32 = jnp.float32
BF16 = jnp.bfloat16


def remote(src, dst, send_sem, recv_sem, device):
    return pltpu.make_async_remote_copy(
        src_ref=src,
        dst_ref=dst,
        send_sem=send_sem,
        recv_sem=recv_sem,
        device_id=device,
        device_id_type=MESH,
    )


def contract(a, b, da, db):
    return lax.dot_general(a, b, (((da,), (db,)), ((), ())), preferred_element_type=F32)


def softmax_terms(score, pos, count, scale, weight):
    logit = jnp.where(count > 0.0, score * scale, -jnp.inf)
    pos_logit = pos * scale
    highest = jnp.maximum(jnp.max(logit, axis=1, keepdims=True), pos_logit)
    neg_exp = count * jnp.exp(logit - highest)
    pos_exp = jnp.exp(pos_logit - highest)
    denominator = jnp.sum(neg_exp, axis=1, keepdims=True) + pos_exp
    row_weight = weight * scale
    return neg_exp * (row_weight / denominator), row_weight * (pos_exp / denominator - 1.0)


def kernel(
    scale_ref, loss_ref, short_ref, send_ref, q_hbm, d_hbm, head_hbm,
    qg_ref, dg_ref, hg_ref,
    rows, head, rows_t, rt_buf, grads,
    out_buf, fetched, back_buf, returned,
    score_buf, part_q, got_q, part_d, got_d, part_h, got_h,
    load_sem, ag_s, ag_r, fe_s, fe_r, sc_s, sc_r, rt_s, rt_r, ba_s, ba_r,
    gq_s, gq_r, gd_s, gd_r, pq_s, pq_r, pd_s, pd_r, hg_s, hg_r,
):
    n_dp, n_mp, ql, cols = 32, 4, 64, 640
    group = 8
    slots = 128
    block = 4
    hrows = 80
    me = lax.axis_index("dp")
    my = lax.axis_index("mp")
    x = me // group
    g = me % group
    feature_total = n_mp * cols
    bounds = [0] + [feature_total // 2 ** (NW - 1 - w) for w in range(NW)]

    def row_block(m):
        return pl.ds(pl.multiple_of(m * cols, cols), cols)

    load_q = pltpu.make_async_copy(q_hbm, rows.at[my, pl.ds(0, ql)], load_sem.at[0])
    load_d = pltpu.make_async_copy(d_hbm, rows.at[my, pl.ds(ql, ql)], load_sem.at[1])
    load_q.start()
    load_d.start()
    order = (0, 1, 3, 2)
    load_h = []
    for k in order:
        src = (my + n_mp - k) % n_mp
        copy = pltpu.make_async_copy(
            head_hbm.at[row_block(src)], head.at[row_block(src)], load_sem.at[2 + k]
        )
        copy.start()
        load_h.append(copy)

    barrier = pltpu.get_barrier_semaphore()
    for k in range(1, n_mp):
        pl.semaphore_signal(
            barrier, inc=1, device_id=(me, (my + k) % n_mp), device_id_type=MESH
        )

    def greet(k, carry):
        pl.semaphore_signal(
            barrier, inc=1, device_id=((me + k) % n_dp, my), device_id_type=MESH
        )
        return carry

    lax.fori_loop(1, n_dp, greet, 0)

    short = short_ref[...]
    lane = lax.broadcasted_iota(jnp.int32, (ql, slots), 1)

    def count_step(j, carry):
        held, total = carry
        for k in range(8):
            now = held if k == 0 else pltpu.roll(held, k, 1)
            total = total + jnp.where(now == lane, 1.0, 0.0)
        return pltpu.roll(held, 8, 1), total

    _, count = lax.fori_loop(0, slots // 8, count_step, (short, jnp.zeros((ql, slots), F32)))
    pick = jnp.where(
        lax.broadcasted_iota(jnp.int32, (ql, slots), 0) == send_ref[...], 1.0, 0.0
    ).astype(BF16)

    load_q.wait()
    load_d.wait()
    pl.semaphore_wait(barrier, n_mp - 1 + n_dp - 1)

    sends = []
    for k in (1, 3, 2):
        copy = remote(
            rows.at[my], rows.at[my], ag_s.at[k], ag_r.at[k], (me, (my + k) % n_mp)
        )
        copy.start()
        sends.append(copy)
    acc = None
    for j, k in enumerate(order):
        src = (my + n_mp - k) % n_mp
        load_h[j].wait()
        if k:
            remote(rows.at[my], rows.at[src], ag_s.at[k], ag_r.at[k], (me, my)).wait_recv()
        term = jnp.dot(rows[src], head[row_block(src), :], preferred_element_type=F32)
        acc = term if acc is None else acc + term
    qp = acc[:ql].astype(BF16)
    dp = acc[ql:].astype(BF16)

    picked = contract(pick, dp, 0, 0).astype(BF16)
    out_buf[...] = picked.reshape(n_dp, block, cols)

    def fetch_send(k, carry):
        peer = (me + k) % n_dp
        remote(out_buf.at[peer], fetched.at[me], fe_s.at[k], fe_r.at[k], (peer, my)).start()
        return carry

    lax.fori_loop(1, n_dp, fetch_send, 0)
    fetched[me] = out_buf[me]

    for m in range(n_mp):
        rows_t[m] = rows[m].T
    for k in range(1, group):
        peer = (g + k) % group
        at = pl.multiple_of(peer * hrows, 16)
        to = pl.multiple_of(g * slots, slots)
        copy = remote(
            rows_t.at[:, pl.ds(at, hrows), :],
            rt_buf.at[:, :, pl.ds(to, slots)],
            rt_s.at[k],
            rt_r.at[k],
            (x * group + peer, my),
        )
        copy.start()
        sends.append(copy)
    rt_buf[:, :, pl.ds(pl.multiple_of(g * slots, slots), slots)] = rows_t[
        :, pl.ds(pl.multiple_of(g * hrows, 16), hrows), :
    ]

    col = lax.broadcasted_iota(jnp.int32, (1, cols), 1)
    seg_col = [
        jnp.where((col >= bounds[s]) & (col < bounds[s + 1]), 1.0, 0.0) for s in range(LOCAL)
    ]
    q_seg = jnp.concatenate([qp * m.astype(BF16) for m in seg_col], axis=0)
    product = qp.astype(F32) * dp.astype(F32)
    pos_prefix = [
        jnp.sum(
            product * jnp.where(col < bounds[s + 1], 1.0, 0.0), axis=1, keepdims=True
        )
        for s in range(LOCAL)
    ]

    def fetch_wait(k, carry):
        src = (me + n_dp - k) % n_dp
        remote(out_buf.at[me], fetched.at[src], fe_s.at[k], fe_r.at[k], (me, my)).wait_recv()
        return carry

    lax.fori_loop(1, n_dp, fetch_wait, 0)
    docs = fetched[...].reshape(slots, cols)
    pieces = contract(q_seg, docs, 1, 1)
    scores = []
    for s in range(LOCAL):
        piece = pieces[s * ql : (s + 1) * ql]
        scores.append(piece if s == 0 else scores[-1] + piece)

    diag = lax.broadcasted_iota(jnp.int32, (ql, slots), 0) == lane
    pos_row = jnp.sum(
        jnp.where(diag, jnp.broadcast_to(pos_prefix[-1], (ql, slots)), 0.0), axis=0, keepdims=True
    )
    score_buf[my, 0:ql, :] = scores[-1]
    score_buf[my, ql : ql + 8, :] = jnp.broadcast_to(pos_row, (8, slots))
    for k in (2, 1, 3):
        copy = remote(
            score_buf.at[my], score_buf.at[my], sc_s.at[k], sc_r.at[k], (me, (my + k) % n_mp)
        )
        copy.start()
        sends.append(copy)

    weight = loss_ref[...]

    def width(w, score, pos):
        scale = scale_ref[w] * (1.0 / math.sqrt(bounds[w + 1]))
        return softmax_terms(score, pos, count, scale, weight[:, w : w + 1])

    narrow = [width(w, scores[w], pos_prefix[w]) for w in range(LOCAL)]
    doc_seg = [docs * m.astype(BF16) for m in seg_col]
    doc_seg = jnp.concatenate(doc_seg, axis=0)

    for k in (1, 3, 2):
        src = (my + n_mp - k) % n_mp
        remote(score_buf.at[my], score_buf.at[src], sc_s.at[k], sc_r.at[k], (me, my)).wait_recv()
    parts = [score_buf[m, 0:ql, :] for m in range(n_mp)]
    pos_parts = [
        jnp.sum(
            jnp.where(diag, jnp.concatenate([score_buf[m, ql : ql + 8, :]] * 8, axis=0), 0.0),
            axis=1,
            keepdims=True,
        )
        for m in range(n_mp)
    ]
    score5, pos5 = parts[0] + parts[1], pos_parts[0] + pos_parts[1]
    neg5, posg5 = width(5, score5, pos5)
    neg6, posg6 = width(6, score5 + (parts[2] + parts[3]), pos5 + (pos_parts[2] + pos_parts[3]))
    run_neg = neg6 + jnp.where(my <= 1, neg5, 0.0)
    run_pos = posg6 + jnp.where(my <= 1, posg5, 0.0)
    coeff = [None] * LOCAL
    pos_cols = jnp.zeros((ql, cols), F32)
    for s in reversed(range(LOCAL)):
        run_neg = run_neg + jnp.where(my == 0, narrow[s][0], 0.0)
        run_pos = run_pos + jnp.where(my == 0, narrow[s][1], 0.0)
        coeff[s] = run_neg.astype(BF16)
        pos_cols = pos_cols + run_pos * seg_col[s]

    by_slot = contract(jnp.concatenate(coeff, axis=0), q_seg, 0, 0).astype(BF16)
    back_buf[...] = by_slot.reshape(n_dp, block, cols)

    def back_send(k, carry):
        peer = (me + k) % n_dp
        remote(back_buf.at[peer], returned.at[me], ba_s.at[k], ba_r.at[k], (peer, my)).start()
        return carry

    lax.fori_loop(1, n_dp, back_send, 0)
    returned[me] = back_buf[me]

    query_back = jnp.dot(jnp.concatenate(coeff, axis=1), doc_seg, preferred_element_type=F32)
    grad_q = (query_back + pos_cols * dp.astype(F32)).astype(BF16)

    partner = x * group + (g + 1 - 2 * (g % 2))

    def spread(first, send_sem, recv_sem, grad):
        at = pl.ds(pl.multiple_of(g * slots + first, ql), ql)
        grads[at, :] = grad
        for k in (4, 2, 6):
            peer = x * group + (g + k) % group
            copy = remote(grads.at[at], grads.at[at], send_sem.at[k], recv_sem.at[k], (peer, my))
            copy.start()
            sends.append(copy)
        copy = remote(grads.at[at], grads.at[at], send_sem.at[0], recv_sem.at[0], (partner, my))
        copy.start()
        sends.append(copy)

    def forward(first, send_sem, recv_sem):
        for k in (2, 6, 4):
            src = (g + group - k) % group
            at = pl.ds(pl.multiple_of(src * slots + first, ql), ql)
            remote(grads.at[at], grads.at[at], send_sem.at[k], recv_sem.at[k], (me, my)).wait_recv()
            copy = remote(
                grads.at[at], grads.at[at], send_sem.at[k + 1], recv_sem.at[k + 1], (partner, my)
            )
            copy.start()
            sends.append(copy)

    def settle(first, send_sem, recv_sem):
        other = g + 1 - 2 * (g % 2)
        for k in (0, 2, 6, 4):
            src = (other + group - k) % group
            at = pl.ds(pl.multiple_of(src * slots + first, ql), ql)
            slot = 0 if k == 0 else k + 1
            remote(
                grads.at[at], grads.at[at], send_sem.at[slot], recv_sem.at[slot], (me, my)
            ).wait_recv()

    def share(grad, part, got, send_sem, recv_sem):
        for k in (2, 1, 3):
            peer = (my + k) % n_mp
            part[k] = contract(grad, head[row_block(peer), :], 1, 1).astype(BF16)
            copy = remote(part.at[k], got.at[k], send_sem.at[k], recv_sem.at[k], (me, peer))
            copy.start()
            sends.append(copy)
        return contract(grad, head[row_block(my), :], 1, 1)

    def gather_parts(own, part, got, send_sem, recv_sem):
        for k in (1, 3, 2):
            remote(part.at[k], got.at[k], send_sem.at[k], recv_sem.at[k], (me, my)).wait_recv()
            own = own + got[k].astype(F32)
        return own

    spread(0, gq_s, gq_r, grad_q)
    own_q = share(grad_q, part_q, got_q, pq_s, pq_r)

    def back_wait(k, carry):
        src = (me + n_dp - k) % n_dp
        remote(back_buf.at[me], returned.at[src], ba_s.at[k], ba_r.at[k], (me, my)).wait_recv()
        return carry

    lax.fori_loop(1, n_dp, back_wait, 0)
    doc_back = jnp.dot(pick, returned[...].reshape(slots, cols), preferred_element_type=F32)
    grad_d = (pos_cols * qp.astype(F32) + doc_back).astype(BF16)
    spread(ql, gd_s, gd_r, grad_d)
    forward(0, gq_s, gq_r)
    own_d = share(grad_d, part_d, got_d, pd_s, pd_r)
    qg_ref[...] = gather_parts(own_q, part_q, got_q, pq_s, pq_r).astype(BF16)

    forward(ql, gd_s, gd_r)
    for k in range(1, group):
        src = (g + group - k) % group
        remote(
            rows_t.at[:, pl.ds(0, hrows), :],
            rt_buf.at[:, :, pl.ds(pl.multiple_of(src * slots, slots), slots)],
            rt_s.at[k],
            rt_r.at[k],
            (me, my),
        ).wait_recv()
    settle(0, gq_s, gq_r)
    settle(ql, gd_s, gd_r)
    everyone = grads[...]
    for k in (2, 1, 3):
        peer = (x + k) % n_mp
        part_h[k] = jnp.dot(rt_buf[peer], everyone, preferred_element_type=F32).astype(BF16)
        copy = remote(
            part_h.at[k], got_h.at[k], hg_s.at[k], hg_r.at[k], (peer * group + g, my)
        )
        copy.start()
        sends.append(copy)
    own_h = jnp.dot(rt_buf[x], everyone, preferred_element_type=F32)
    dg_ref[...] = gather_parts(own_d, part_d, got_d, pd_s, pd_r).astype(BF16)
    hg_ref[...] = gather_parts(own_h, part_h, got_h, hg_s, hg_r)

    def drain(k, carry):
        peer = (me + k) % n_dp
        remote(out_buf.at[peer], fetched.at[me], fe_s.at[k], fe_r.at[k], (peer, my)).wait_send()
        remote(back_buf.at[peer], returned.at[me], ba_s.at[k], ba_r.at[k], (peer, my)).wait_send()
        return carry

    lax.fori_loop(1, n_dp, drain, 0)
    for copy in sends:
        copy.wait_send()


def on_device(query_rows, doc_rows, head, logit_scale, loss_grad, shortlist, send_rows):
    ql, cols = query_rows.shape
    dma = pltpu.SemaphoreType.DMA
    vmem = pl.BlockSpec(memory_space=pltpu.VMEM)
    hbm = pl.BlockSpec(memory_space=pl.ANY)
    return pl.pallas_call(
        kernel,
        out_shape=(
            jax.ShapeDtypeStruct((ql, cols), BF16),
            jax.ShapeDtypeStruct((ql, cols), BF16),
            jax.ShapeDtypeStruct((80, cols), F32),
        ),
        in_specs=[pl.BlockSpec(memory_space=pltpu.SMEM), vmem, vmem, vmem, hbm, hbm, hbm],
        out_specs=(vmem, vmem, vmem),
        scratch_shapes=[
            pltpu.VMEM((4, 2 * ql, cols), BF16),
            pltpu.VMEM((4 * cols, cols), BF16),
            pltpu.VMEM((4, cols, 2 * ql), BF16),
            pltpu.VMEM((4, 80, 1024), BF16),
            pltpu.VMEM((1024, cols), BF16),
            pltpu.VMEM((32, 4, cols), BF16),
            pltpu.VMEM((32, 4, cols), BF16),
            pltpu.VMEM((32, 4, cols), BF16),
            pltpu.VMEM((32, 4, cols), BF16),
            pltpu.VMEM((4, ql + 8, 128), F32),
            pltpu.VMEM((4, ql, cols), BF16),
            pltpu.VMEM((4, ql, cols), BF16),
            pltpu.VMEM((4, ql, cols), BF16),
            pltpu.VMEM((4, ql, cols), BF16),
            pltpu.VMEM((4, 80, cols), BF16),
            pltpu.VMEM((4, 80, cols), BF16),
            dma((6,)), dma((4,)), dma((4,)), dma((32,)), dma((32,)), dma((4,)), dma((4,)),
            dma((8,)), dma((8,)), dma((32,)), dma((32,)),
            dma((8,)), dma((8,)), dma((8,)), dma((8,)),
            dma((4,)), dma((4,)), dma((4,)), dma((4,)), dma((4,)), dma((4,)),
        ],
        compiler_params=pltpu.CompilerParams(
            collective_id=0, has_side_effects=True, vmem_limit_bytes=48 * 1024 * 1024
        ),
    )(logit_scale, loss_grad, shortlist, send_rows, query_rows, doc_rows, head)


def solution(mesh):
    placed = (
        P("dp", "mp"),
        P("dp", "mp"),
        P(None, "mp"),
        P(),
        P("dp", None),
        P("dp", None),
        P("dp", None),
    )
    return jax.shard_map(
        on_device,
        mesh=mesh,
        in_specs=placed,
        out_specs=(P("dp", "mp"), P("dp", "mp"), P("dp", "mp")),
        check_vma=False,
    )
```

time: 180 us -> 63.9 us (0.35)
  blocking collectives: 60.1 us -> 0 us
  Pallas kernels: 0 us -> 54.5 us
  waiting for transfers between devices: 34.9 us -> 0 us
  matrix products: 27.6 us -> 0 us
  starting transfers between devices: 23 us -> 0 us
  between operations: 14.4 us -> 0.65 us
  other arithmetic: 8.45 us -> 0 us
    all_gather x2 -> x0, blocking collectives: 60.1 us -> none  [in_one_piece(): filled = lax.all_gather(both, axis, axis=dim, tiled=True)]
    pallas_call x0 -> x1, Pallas kernels: none -> 54.5 us  [on_device(): pl.pallas_call(kernel, out_shape=(jax.ShapeDtypeStruct((ql, cols), BF16),...]
    dot_general x13 -> x0, matrix products: 27.6 us -> none  [the longest x1 5.67 us: on_device(): lax.dot_general(whole_doc, grad_doc, row_contract, preferred_element_type...]
    all_to_all x4 -> x0, waiting for transfers between devices: 23.6 us -> none  [the longest x1 13.2 us: from_everyone(): return lax.all_to_all(copies, axis, split_axis=0, concat_axis=0, tiled=True)]
    all_to_all x4 -> x0, starting transfers between devices: 23 us -> none  [the longest x1 9.93 us: on_device(): lax.all_to_all(outgoing, 'dp', split_axis=0, concat_axis=0, tiled=True)]
    reduce_scatter x1 -> x0, waiting for transfers between devices: 11.3 us -> none  [on_device(): lax.psum_scatter((query_term + doc_term).astype(jnp.bfloat16), 'dp', scat...]
    unnamed x12 -> x16, local copies, waits for them, and re-layouts: 1.71 us -> 8.49 us
    all_to_all x4 -> x0, local copies, waits for them, and re-layouts: 5.17 us -> none  [the longest x1 4.19 us: on_device(): lax.all_to_all(head, 'mp', split_axis=0, concat_axis=1, tiled=True)]
  transfers between devices with their start and end apart: 5 -> 0, of which waited for: 4 -> 0; matrix products, arithmetic and copies ran while one was open for 8% -> 0% of each run, Pallas kernels for 0% -> 0%
where the time goes in v1:
time: 63.9 us; the launch traced here: 63.6 us
  Pallas kernels  54.5 us (85%)
  local copies, waits for them, and re-layouts  8.49 us (13%)
  between operations  0.65 us (1%)
    pallas_call x1, Pallas kernels, on_device(): pl.pallas_call(kernel, out_shape=(jax.ShapeDtypeStruct((ql, cols), BF16),...  54.5 us
    unnamed x16, local copies, waits for them, and re-layouts  8.49 us

profile of v1, /device:TPU:1, one launch (start us, length us, event | category | flops | bytes accessed | tf_op | source)
XLA Modules:
  0.0 63.6 jit_solution(1026187505489643199)
XLA Ops:
  0.6 0.8 %copy.10.loss_ref = f32[64,7]{1,0:T(8,128)S(1)} copy(f32[64,7]{0,1:T(8,128)} %param.11) | data formatting | bytes 3584 | tf_op args[4]
  1.4 0.0 copy-start
  1.4 1.9 %copy-done = bf16[2560,640]{1,0:T(8,128)(2,1)S(1)} copy-done((bf16[2560,640]{1,0:T(8,128)(2,1)S(1)}, bf16[2560,640]{1,0:T(8,128)(2,1)}, u32[]{:S(2)}) %copy-start) | copy-done | bytes 3276824
  3.3 0.0 copy-start.1
  3.3 0.9 %copy-done.1 = bf16[64,640]{1,0:T(8,128)(2,1)S(1)} copy-done((bf16[64,640]{1,0:T(8,128)(2,1)S(1)}, bf16[64,640]{1,0:T(8,128)(2,1)}, u32[]{:S(2)}) %copy-start.1) | copy-done | bytes 81944
  4.2 0.0 copy-start.2
  4.2 0.9 %copy-done.2 = bf16[64,640]{1,0:T(8,128)(2,1)S(1)} copy-done((bf16[64,640]{1,0:T(8,128)(2,1)S(1)}, bf16[64,640]{1,0:T(8,128)(2,1)}, u32[]{:S(2)}) %copy-start.2) | copy-done | bytes 81944
  5.1 0.0 copy-start.3
  5.1 0.8 %copy-done.3 = s32[64,128]{1,0:T(8,128)S(1)} copy-done((s32[64,128]{1,0:T(8,128)S(1)}, s32[64,128]{1,0:T(8,128)}, u32[]{:S(2)}) %copy-start.3) | copy-done | bytes 32792
  5.9 0.0 copy-start.4
  5.9 0.7 %copy-done.4 = f32[7]{0:T(128)S(1)} copy-done((f32[7]{0:T(128)S(1)}, f32[7]{0:T(128)}, u32[]{:S(2)}) %copy-start.4) | copy-done | bytes 52
  6.5 0.0 copy-start.5
  6.5 0.7 %copy-done.5 = s32[1,128]{1,0:T(1,128)S(1)} copy-done((s32[1,128]{1,0:T(1,128)S(1)}, s32[1,128]{1,0:T(1,128)}, u32[]{:S(2)}) %copy-start.5) | copy-done | bytes 536
  7.2 54.5 %shard_map.94 = (bf16[64,640]{1,0:T(8,128)(2,1)S(1)}, bf16[64,640]{1,0:T(8,128)(2,1)S(1)}, f32[80,640]{1,0:T(8,128)S(1)}) custom-call(f32[7]{0:T(128)S(1)} %copy-done.4, f32[64,7]{1,0:T(8,128)S(1)} %copy.10.loss_ref, s32[64,128]{1,0:T(8,128)S(1)} %copy-done.3, s32[1,128]{1,0:T(1,128)S(1)} %copy-done.5, bf16[64,640]{1,0:T(8,128)(2,1)S(1)} %copy-done.1, ...), custom_call_target="tpu_custom_call" | custom-call | tf_op jit(solution)/shard_map/pallas_call | solution.py:358
  61.6 0.6 %copy.14 = bf16[64,640]{1,0:T(8,128)(2,1)} copy(bf16[64,640]{1,0:T(8,128)(2,1)S(1)} %get-tuple-element.6) | data formatting | bytes 163840
  62.3 0.6 copy.15
  62.9 0.7 %copy.16 = f32[80,640]{1,0:T(8,128)} copy(f32[80,640]{1,0:T(8,128)S(1)} %get-tuple-element.8) | data formatting | bytes 409600
Async XLA Ops:
  1.4 1.9 %copy-start = (bf16[2560,640]{1,0:T(8,128)(2,1)S(1)}, bf16[2560,640]{1,0:T(8,128)(2,1)}, u32[]{:S(2)}) copy-start(bf16[2560,640]{1,0:T(8,128)(2,1)} %head_hbm.1) | copy-start | bytes 9830404
  3.3 0.9 %copy-start.1 = (bf16[64,640]{1,0:T(8,128)(2,1)S(1)}, bf16[64,640]{1,0:T(8,128)(2,1)}, u32[]{:S(2)}) copy-start(bf16[64,640]{1,0:T(8,128)(2,1)} %q_hbm.1) | copy-start | bytes 245764
  4.2 0.9 %copy-start.2 = (bf16[64,640]{1,0:T(8,128)(2,1)S(1)}, bf16[64,640]{1,0:T(8,128)(2,1)}, u32[]{:S(2)}) copy-start(bf16[64,640]{1,0:T(8,128)(2,1)} %d_hbm.1) | copy-start | bytes 245764
  5.1 0.8 %copy-start.3 = (s32[64,128]{1,0:T(8,128)S(1)}, s32[64,128]{1,0:T(8,128)}, u32[]{:S(2)}) copy-start(s32[64,128]{1,0:T(8,128)} %short_ref.1) | copy-start | bytes 98308
  5.9 0.7 %copy-start.4 = (f32[7]{0:T(128)S(1)}, f32[7]{0:T(128)}, u32[]{:S(2)}) copy-start(f32[7]{0:T(128)} %scale_ref.1) | copy-start | bytes 88
  6.5 0.7 %copy-start.5 = (s32[1,128]{1,0:T(1,128)S(1)}, s32[1,128]{1,0:T(1,128)}, u32[]{:S(2)}) copy-start(s32[1,128]{1,0:T(1,128)} %send_ref.1) | copy-start | bytes 1540

commit v2 on v1

--- a/solution.py
+++ b/solution.py
@@ -26,6 +26,18 @@
     )
 
 
+class Phases:
+    def __init__(self):
+        self.open = None
+
+    def __call__(self, name):
+        if self.open is not None:
+            self.open.__exit__(None, None, None)
+        self.open = jax.named_scope(name) if name else None
+        if self.open is not None:
+            self.open.__enter__()
+
+
 def contract(a, b, da, db):
     return lax.dot_general(a, b, (((da,), (db,)), ((), ())), preferred_element_type=F32)
 
@@ -42,9 +54,9 @@
 
 
 def kernel(
-    scale_ref, loss_ref, short_ref, send_ref, q_hbm, d_hbm, head_hbm,
+    scale_hbm, loss_hbm, short_hbm, send_hbm, q_hbm, d_hbm, head_hbm,
     qg_ref, dg_ref, hg_ref,
-    rows, head, rows_t, rt_buf, grads,
+    scale_ref, loss_ref, short_ref, send_ref, rows, head, rows_t, rt_buf, grads,
     out_buf, fetched, back_buf, returned,
     score_buf, part_q, got_q, part_d, got_d, part_h, got_h,
     load_sem, ag_s, ag_r, fe_s, fe_r, sc_s, sc_r, rt_s, rt_r, ba_s, ba_r,
@@ -65,10 +77,20 @@
     def row_block(m):
         return pl.ds(pl.multiple_of(m * cols, cols), cols)
 
+    phase = Phases()
+    phase("loads")
     load_q = pltpu.make_async_copy(q_hbm, rows.at[my, pl.ds(0, ql)], load_sem.at[0])
     load_d = pltpu.make_async_copy(d_hbm, rows.at[my, pl.ds(ql, ql)], load_sem.at[1])
+    load_short = pltpu.make_async_copy(short_hbm, short_ref, load_sem.at[6])
+    load_send = pltpu.make_async_copy(send_hbm, send_ref, load_sem.at[7])
+    load_loss = pltpu.make_async_copy(loss_hbm, loss_ref, load_sem.at[8])
+    load_scale = pltpu.make_async_copy(scale_hbm, scale_ref, load_sem.at[9])
+    load_d.start()
     load_q.start()
-    load_d.start()
+    load_short.start()
+    load_send.start()
+    load_loss.start()
+    load_scale.start()
     order = (0, 1, 3, 2)
     load_h = []
     for k in order:
@@ -79,60 +101,142 @@
         copy.start()
         load_h.append(copy)
 
+    phase("greet")
     barrier = pltpu.get_barrier_semaphore()
     for k in range(1, n_mp):
         pl.semaphore_signal(
             barrier, inc=1, device_id=(me, (my + k) % n_mp), device_id_type=MESH
         )
 
-    def greet(k, carry):
+    for k in range(1, n_dp):
         pl.semaphore_signal(
             barrier, inc=1, device_id=((me + k) % n_dp, my), device_id_type=MESH
         )
-        return carry
-
-    lax.fori_loop(1, n_dp, greet, 0)
-
-    short = short_ref[...]
-    lane = lax.broadcasted_iota(jnp.int32, (ql, slots), 1)
-
-    def count_step(j, carry):
-        held, total = carry
-        for k in range(8):
-            now = held if k == 0 else pltpu.roll(held, k, 1)
-            total = total + jnp.where(now == lane, 1.0, 0.0)
-        return pltpu.roll(held, 8, 1), total
-
-    _, count = lax.fori_loop(0, slots // 8, count_step, (short, jnp.zeros((ql, slots), F32)))
+
+    phase("pick_map")
+    load_send.wait()
     pick = jnp.where(
         lax.broadcasted_iota(jnp.int32, (ql, slots), 0) == send_ref[...], 1.0, 0.0
     ).astype(BF16)
 
+    load_loss.wait()
+    load_scale.wait()
+    weight = loss_ref[...].T
+    phase("barrier")
     load_q.wait()
     load_d.wait()
+    rows_t[...] = rows[my].T
+    mine = pl.ds(pl.multiple_of(g * slots, slots), slots)
+    rt_buf[my, :, mine] = rows_t[pl.ds(pl.multiple_of(g * hrows, 16), hrows), :]
     pl.semaphore_wait(barrier, n_mp - 1 + n_dp - 1)
 
+    right, left = (my + 1) % n_mp, (my + n_mp - 1) % n_mp
+    far = (my + 2) % n_mp
+    half = ql // 2
     sends = []
-    for k in (1, 3, 2):
+
+    def row_copy(part, way, piece, src):
+        second = (way == 1) if piece == 2 else (piece == 1)
+        at = pl.ds((1 - part) * ql + (half if second else 0), half)
+        slot = part * 6 + way * 3 + piece
+        return remote(
+            rows.at[src, at], rows.at[src, at], ag_s.at[slot], ag_r.at[slot],
+            (me, right if way == 0 else left),
+        )
+
+    def rows_start(part):
+        for way, piece in ((0, 0), (1, 1), (0, 1), (1, 0)):
+            copy = row_copy(part, way, piece, my)
+            copy.start()
+            sends.append(copy)
+
+    def rows_relay(part):
+        for way, src in ((0, left), (1, right)):
+            row_copy(part, way, way, src).wait_recv()
+            copy = row_copy(part, way, 2, src)
+            copy.start()
+            sends.append(copy)
+
+    def rows_rest(part):
+        row_copy(part, 0, 1, left).wait_recv()
+        yield left
+        row_copy(part, 1, 0, right).wait_recv()
+        yield right
+        row_copy(part, 0, 2, far).wait_recv()
+        row_copy(part, 1, 2, far).wait_recv()
+        yield far
+
+    def product_of(part, src):
+        at = (1 - part) * ql
+        return jnp.dot(
+            rows[src, at : at + ql, :], head[row_block(src), :], preferred_element_type=F32
+        )
+
+    def turn_copy(way, piece, src):
+        second = (way == 1) if piece == 2 else (piece == 1)
+        at = pl.ds(512 if second else 0, 512)
+        slot = 8 + way * 3 + piece
+        return remote(
+            rt_buf.at[src, :, at], rt_buf.at[src, :, at], rt_s.at[slot], rt_r.at[slot],
+            (me, right if way == 0 else left),
+        )
+
+    def turn_start():
+        for k in range(1, group):
+            src = (g + group - k) % group
+            remote(
+                rows_t.at[pl.ds(0, hrows)],
+                rt_buf.at[my, :, pl.ds(pl.multiple_of(src * slots, slots), slots)],
+                rt_s.at[k],
+                rt_r.at[k],
+                (me, my),
+            ).wait_recv()
+        for way, piece in ((0, 0), (1, 1), (0, 1), (1, 0)):
+            copy = turn_copy(way, piece, my)
+            copy.start()
+            sends.append(copy)
+
+    def turn_relay():
+        for way, src in ((0, left), (1, right)):
+            turn_copy(way, way, src).wait_recv()
+            copy = turn_copy(way, 2, src)
+            copy.start()
+            sends.append(copy)
+
+    def turn_rest():
+        turn_copy(0, 1, left).wait_recv()
+        turn_copy(1, 0, right).wait_recv()
+        turn_copy(0, 2, far).wait_recv()
+        turn_copy(1, 2, far).wait_recv()
+
+    phase("rows_d")
+    rows_start(0)
+    for k in range(1, group):
+        peer = (g + k) % group
         copy = remote(
-            rows.at[my], rows.at[my], ag_s.at[k], ag_r.at[k], (me, (my + k) % n_mp)
+            rows_t.at[pl.ds(pl.multiple_of(peer * hrows, 16), hrows)],
+            rt_buf.at[my, :, mine],
+            rt_s.at[k],
+            rt_r.at[k],
+            (x * group + peer, my),
         )
         copy.start()
         sends.append(copy)
-    acc = None
-    for j, k in enumerate(order):
-        src = (my + n_mp - k) % n_mp
-        load_h[j].wait()
-        if k:
-            remote(rows.at[my], rows.at[src], ag_s.at[k], ag_r.at[k], (me, my)).wait_recv()
-        term = jnp.dot(rows[src], head[row_block(src), :], preferred_element_type=F32)
-        acc = term if acc is None else acc + term
-    qp = acc[:ql].astype(BF16)
-    dp = acc[ql:].astype(BF16)
+    load_h[0].wait()
+    acc = product_of(0, my)
+    rows_relay(0)
+    rows_start(1)
+    for copy in load_h[1:]:
+        copy.wait()
+    for src in rows_rest(0):
+        acc = acc + product_of(0, src)
+    phase("pick")
+    dp = acc.astype(BF16)
 
     picked = contract(pick, dp, 0, 0).astype(BF16)
     out_buf[...] = picked.reshape(n_dp, block, cols)
 
+    phase("fetch")
     def fetch_send(k, carry):
         peer = (me + k) % n_dp
         remote(out_buf.at[peer], fetched.at[me], fe_s.at[k], fe_r.at[k], (peer, my)).start()
@@ -141,25 +245,23 @@
     lax.fori_loop(1, n_dp, fetch_send, 0)
     fetched[me] = out_buf[me]
 
-    for m in range(n_mp):
-        rows_t[m] = rows[m].T
-    for k in range(1, group):
-        peer = (g + k) % group
-        at = pl.multiple_of(peer * hrows, 16)
-        to = pl.multiple_of(g * slots, slots)
-        copy = remote(
-            rows_t.at[:, pl.ds(at, hrows), :],
-            rt_buf.at[:, :, pl.ds(to, slots)],
-            rt_s.at[k],
-            rt_r.at[k],
-            (x * group + peer, my),
-        )
-        copy.start()
-        sends.append(copy)
-    rt_buf[:, :, pl.ds(pl.multiple_of(g * slots, slots), slots)] = rows_t[
-        :, pl.ds(pl.multiple_of(g * hrows, 16), hrows), :
-    ]
-
+    phase("relay_q")
+    rows_relay(1)
+    phase("count")
+    load_short.wait()
+    short = short_ref[...]
+    lane = lax.broadcasted_iota(jnp.int32, (ql, slots), 1)
+
+    count = jnp.zeros((ql, slots), F32)
+    for k in range(slots):
+        count = count + jnp.where((short if k == 0 else pltpu.roll(short, k, 1)) == lane, 1.0, 0.0)
+    phase("rows_q")
+    acc = product_of(1, my)
+    for src in rows_rest(1):
+        acc = acc + product_of(1, src)
+    qp = acc.astype(BF16)
+
+    phase("mask")
     col = lax.broadcasted_iota(jnp.int32, (1, cols), 1)
     seg_col = [
         jnp.where((col >= bounds[s]) & (col < bounds[s + 1]), 1.0, 0.0) for s in range(LOCAL)
@@ -173,12 +275,14 @@
         for s in range(LOCAL)
     ]
 
+    phase("fetch_wait")
     def fetch_wait(k, carry):
         src = (me + n_dp - k) % n_dp
         remote(out_buf.at[me], fetched.at[src], fe_s.at[k], fe_r.at[k], (me, my)).wait_recv()
         return carry
 
     lax.fori_loop(1, n_dp, fetch_wait, 0)
+    phase("score")
     docs = fetched[...].reshape(slots, cols)
     pieces = contract(q_seg, docs, 1, 1)
     scores = []
@@ -199,8 +303,7 @@
         copy.start()
         sends.append(copy)
 
-    weight = loss_ref[...]
-
+    phase("narrow")
     def width(w, score, pos):
         scale = scale_ref[w] * (1.0 / math.sqrt(bounds[w + 1]))
         return softmax_terms(score, pos, count, scale, weight[:, w : w + 1])
@@ -209,9 +312,12 @@
     doc_seg = [docs * m.astype(BF16) for m in seg_col]
     doc_seg = jnp.concatenate(doc_seg, axis=0)
 
+    phase("score_wait")
     for k in (1, 3, 2):
         src = (my + n_mp - k) % n_mp
         remote(score_buf.at[my], score_buf.at[src], sc_s.at[k], sc_r.at[k], (me, my)).wait_recv()
+    turn_start()
+    phase("wide")
     parts = [score_buf[m, 0:ql, :] for m in range(n_mp)]
     pos_parts = [
         jnp.sum(
@@ -234,6 +340,7 @@
         coeff[s] = run_neg.astype(BF16)
         pos_cols = pos_cols + run_pos * seg_col[s]
 
+    phase("by_slot")
     by_slot = contract(jnp.concatenate(coeff, axis=0), q_seg, 0, 0).astype(BF16)
     back_buf[...] = by_slot.reshape(n_dp, block, cols)
 
@@ -245,6 +352,7 @@
     lax.fori_loop(1, n_dp, back_send, 0)
     returned[me] = back_buf[me]
 
+    phase("grad_q")
     query_back = jnp.dot(jnp.concatenate(coeff, axis=1), doc_seg, preferred_element_type=F32)
     grad_q = (query_back + pos_cols * dp.astype(F32)).astype(BF16)
 
@@ -298,34 +406,39 @@
             own = own + got[k].astype(F32)
         return own
 
+    phase("spread_q")
     spread(0, gq_s, gq_r, grad_q)
+    phase("turn_relay")
+    turn_relay()
+    phase("share_q")
     own_q = share(grad_q, part_q, got_q, pq_s, pq_r)
 
+    phase("back_wait")
     def back_wait(k, carry):
         src = (me + n_dp - k) % n_dp
         remote(back_buf.at[me], returned.at[src], ba_s.at[k], ba_r.at[k], (me, my)).wait_recv()
         return carry
 
     lax.fori_loop(1, n_dp, back_wait, 0)
+    phase("grad_d")
     doc_back = jnp.dot(pick, returned[...].reshape(slots, cols), preferred_element_type=F32)
     grad_d = (pos_cols * qp.astype(F32) + doc_back).astype(BF16)
     spread(ql, gd_s, gd_r, grad_d)
+    phase("forward_q")
     forward(0, gq_s, gq_r)
+    phase("share_d")
     own_d = share(grad_d, part_d, got_d, pd_s, pd_r)
+    phase("query_out")
     qg_ref[...] = gather_parts(own_q, part_q, got_q, pq_s, pq_r).astype(BF16)
 
+    phase("forward_d")
     forward(ql, gd_s, gd_r)
-    for k in range(1, group):
-        src = (g + group - k) % group
-        remote(
-            rows_t.at[:, pl.ds(0, hrows), :],
-            rt_buf.at[:, :, pl.ds(pl.multiple_of(src * slots, slots), slots)],
-            rt_s.at[k],
-            rt_r.at[k],
-            (me, my),
-        ).wait_recv()
+    phase("rt_wait")
+    turn_rest()
+    phase("settle")
     settle(0, gq_s, gq_r)
     settle(ql, gd_s, gd_r)
+    phase("head")
     everyone = grads[...]
     for k in (2, 1, 3):
         peer = (x + k) % n_mp
@@ -336,9 +449,12 @@
         copy.start()
         sends.append(copy)
     own_h = jnp.dot(rt_buf[x], everyone, preferred_element_type=F32)
+    phase("doc_out")
     dg_ref[...] = gather_parts(own_d, part_d, got_d, pd_s, pd_r).astype(BF16)
+    phase("head_out")
     hg_ref[...] = gather_parts(own_h, part_h, got_h, hg_s, hg_r)
 
+    phase("drain")
     def drain(k, carry):
         peer = (me + k) % n_dp
         remote(out_buf.at[peer], fetched.at[me], fe_s.at[k], fe_r.at[k], (peer, my)).wait_send()
@@ -348,13 +464,15 @@
     lax.fori_loop(1, n_dp, drain, 0)
     for copy in sends:
         copy.wait_send()
+    phase(None)
 
 
 def on_device(query_rows, doc_rows, head, logit_scale, loss_grad, shortlist, send_rows):
     ql, cols = query_rows.shape
     dma = pltpu.SemaphoreType.DMA
     vmem = pl.BlockSpec(memory_space=pltpu.VMEM)
-    hbm = pl.BlockSpec(memory_space=pl.ANY)
+    hbm = pl.BlockSpec(memory_space=pltpu.HBM)
+    operands = (logit_scale, loss_grad.T, shortlist, send_rows, query_rows, doc_rows, head)
     return pl.pallas_call(
         kernel,
         out_shape=(
@@ -362,12 +480,16 @@
             jax.ShapeDtypeStruct((ql, cols), BF16),
             jax.ShapeDtypeStruct((80, cols), F32),
         ),
-        in_specs=[pl.BlockSpec(memory_space=pltpu.SMEM), vmem, vmem, vmem, hbm, hbm, hbm],
+        in_specs=[hbm] * 7,
         out_specs=(vmem, vmem, vmem),
         scratch_shapes=[
+            pltpu.SMEM((NW,), F32),
+            pltpu.VMEM((NW, ql), F32),
+            pltpu.VMEM((ql, 128), jnp.int32),
+            pltpu.VMEM((1, 128), jnp.int32),
             pltpu.VMEM((4, 2 * ql, cols), BF16),
             pltpu.VMEM((4 * cols, cols), BF16),
-            pltpu.VMEM((4, cols, 2 * ql), BF16),
+            pltpu.VMEM((cols, 2 * ql), BF16),
             pltpu.VMEM((4, 80, 1024), BF16),
             pltpu.VMEM((1024, cols), BF16),
             pltpu.VMEM((32, 4, cols), BF16),
@@ -381,15 +503,15 @@
             pltpu.VMEM((4, ql, cols), BF16),
             pltpu.VMEM((4, 80, cols), BF16),
             pltpu.VMEM((4, 80, cols), BF16),
-            dma((6,)), dma((4,)), dma((4,)), dma((32,)), dma((32,)), dma((4,)), dma((4,)),
-            dma((8,)), dma((8,)), dma((32,)), dma((32,)),
+            dma((10,)), dma((12,)), dma((12,)), dma((32,)), dma((32,)), dma((4,)), dma((4,)),
+            dma((14,)), dma((14,)), dma((32,)), dma((32,)),
             dma((8,)), dma((8,)), dma((8,)), dma((8,)),
             dma((4,)), dma((4,)), dma((4,)), dma((4,)), dma((4,)), dma((4,)),
         ],
         compiler_params=pltpu.CompilerParams(
             collective_id=0, has_side_effects=True, vmem_limit_bytes=48 * 1024 * 1024
         ),
-    )(logit_scale, loss_grad, shortlist, send_rows, query_rows, doc_rows, head)
+    )(*[pltpu.with_memory_space_constraint(a, pltpu.HBM) for a in operands])
 
 
 def solution(mesh):

time: 63.9 us -> 53 us (0.83)
  local copies, waits for them, and re-layouts: 8.49 us -> 1.95 us
  Pallas kernels: 54.5 us -> 50.3 us
    unnamed x16 -> x3, local copies, waits for them, and re-layouts: 8.49 us -> 1.95 us
    pallas_call x1, Pallas kernels: 54.5 us -> 50.3 us  [on_device(): pl.pallas_call(kernel, out_shape=(jax.ShapeDtypeStruct((ql, cols), BF16),...]
where the time goes in v2:
time: 53 us; the launch traced here: 52.9 us
  Pallas kernels  50.3 us (95%)
  local copies, waits for them, and re-layouts  1.95 us (4%)
  between operations  0.64 us (1%)
    pallas_call x1, Pallas kernels, on_device(): pl.pallas_call(kernel, out_shape=(jax.ShapeDtypeStruct((ql, cols), BF16),...  50.3 us
    unnamed x3, local copies, waits for them, and re-layouts  1.95 us

profile of v2, /device:TPU:1, one launch (start us, length us, event | category | flops | bytes accessed | tf_op | source)
XLA Modules:
  0.0 52.9 jit_solution(16465523831522620597)
XLA Ops:
  0.6 50.3 %shard_map.94 = (bf16[64,640]{1,0:T(8,128)(2,1)S(1)}, bf16[64,640]{1,0:T(8,128)(2,1)S(1)}, f32[80,640]{1,0:T(8,128)S(1)}) custom-call(f32[7]{0:T(128)} %scale_hbm.1, f32[7,64]{1,0:T(8,128)} %bitcast.1, s32[64,128]{1,0:T(8,128)} %short_hbm.1, s32[1,128]{1,0:T(1,128)} %send_hbm.1, bf16[64,640]{1,0:T(8,128)(2,1)} %q_hbm.1, bf16[64,640]{1,0:T(8,128)(2,1)} %d_hbm.1, ...), custom_call_target="tpu_custom_call" | custom-call | tf_op jit(solution)/shard_map/pallas_call | solution.py:476
  51.0 0.6 %copy.13 = bf16[64,640]{1,0:T(8,128)(2,1)} copy(bf16[64,640]{1,0:T(8,128)(2,1)S(1)} %get-tuple-element.6) | data formatting | bytes 163840
  51.6 0.6 %copy.14 = bf16[64,640]{1,0:T(8,128)(2,1)} copy(bf16[64,640]{1,0:T(8,128)(2,1)S(1)} %get-tuple-element.7) | data formatting | bytes 163840
  52.2 0.7 %copy.15 = f32[80,640]{1,0:T(8,128)} copy(f32[80,640]{1,0:T(8,128)S(1)} %get-tuple-element.8) | data formatting | bytes 409600

commit v3 on v2

v3 whole, which is shorter than its diff:
```python
import functools
import math

import jax
import jax.numpy as jnp
from jax import lax
from jax.experimental import pallas as pl
from jax.experimental.pallas import tpu as pltpu
from jax.sharding import PartitionSpec as P

NW = 7
LOCAL = 5
MESH = pl.DeviceIdType.MESH
F32 = jnp.float32
BF16 = jnp.bfloat16


def remote(src, dst, send_sem, recv_sem, device):
    return pltpu.make_async_remote_copy(
        src_ref=src,
        dst_ref=dst,
        send_sem=send_sem,
        recv_sem=recv_sem,
        device_id=device,
        device_id_type=MESH,
    )


class Phases:
    def __init__(self):
        self.open = None

    def __call__(self, name):
        if self.open is not None:
            self.open.__exit__(None, None, None)
        self.open = jax.named_scope(name) if name else None
        if self.open is not None:
            self.open.__enter__()


def contract(a, b, da, db):
    return lax.dot_general(a, b, (((da,), (db,)), ((), ())), preferred_element_type=F32)


def softmax_terms(score, pos, count, scale, weight):
    logit = jnp.where(count > 0.0, score * scale, -jnp.inf)
    pos_logit = pos * scale
    highest = jnp.maximum(jnp.max(logit, axis=1, keepdims=True), pos_logit)
    neg_exp = count * jnp.exp(logit - highest)
    pos_exp = jnp.exp(pos_logit - highest)
    denominator = jnp.sum(neg_exp, axis=1, keepdims=True) + pos_exp
    row_weight = weight * scale
    return neg_exp * (row_weight / denominator), row_weight * (pos_exp / denominator - 1.0)


def kernel(
    scale_hbm, loss_hbm, short_hbm, send_hbm, q_hbm, d_hbm, head_hbm,
    qg_hbm, dg_hbm, hg_hbm,
    qg_ref, dg_ref, hg_ref,
    scale_ref, loss_ref, short_ref, send_ref, rows, head, rows_t, rt_buf, grads,
    out_buf, fetched, back_buf, returned,
    score_buf, part_q, got_q, part_d, got_d, full_h, part_h, got_h,
    load_sem, ag_s, ag_r, fe_s, fe_r, sc_s, sc_r, rt_s, rt_r, ba_s, ba_r,
    gr_s, gr_r, gp_r, pq_s, pq_r, pd_s, pd_r, hg_s, hg_r, word,
):
    n_dp, n_mp, ql, cols = 32, 4, 64, 640
    group = 8
    slots = 128
    block = 4
    hrows = 40
    me = lax.axis_index("dp")
    my = lax.axis_index("mp")
    x = me // group
    g = me % group
    z = g // 2
    feature_total = n_mp * cols
    bounds = [0] + [feature_total // 2 ** (NW - 1 - w) for w in range(NW)]

    def row_block(m):
        return pl.ds(pl.multiple_of(m * cols, cols), cols)

    phase = Phases()
    phase("loads")
    load_q = pltpu.make_async_copy(q_hbm, rows.at[my, pl.ds(0, ql)], load_sem.at[0])
    load_d = pltpu.make_async_copy(d_hbm, rows.at[my, pl.ds(ql, ql)], load_sem.at[1])
    load_short = pltpu.make_async_copy(short_hbm, short_ref, load_sem.at[6])
    load_send = pltpu.make_async_copy(send_hbm, send_ref, load_sem.at[7])
    load_loss = pltpu.make_async_copy(loss_hbm, loss_ref, load_sem.at[8])
    load_scale = pltpu.make_async_copy(scale_hbm, scale_ref, load_sem.at[9])
    load_d.start()
    load_q.start()
    load_short.start()
    load_send.start()
    load_loss.start()
    load_scale.start()
    order = (0, 1, 3, 2)
    load_h = []
    for k in order:
        src = (my + n_mp - k) % n_mp
        copy = pltpu.make_async_copy(
            head_hbm.at[row_block(src)], head.at[row_block(src)], load_sem.at[2 + k]
        )
        copy.start()
        load_h.append(copy)

    phase("greet")
    right, left = (my + 1) % n_mp, (my + n_mp - 1) % n_mp
    far = (my + 2) % n_mp
    core = me % 2
    partner = me + 1 - 2 * core
    x_near = ((me + group) % n_dp, (me + n_dp - group) % n_dp)
    z_near = (x * group + (g + 2) % group, x * group + (g + 6) % group)
    barrier = pltpu.get_barrier_semaphore()
    near = [(me, right), (me, left), (me, far), (partner, my)]
    near += [(peer, my) for peer in x_near + z_near]
    for device in near:
        pl.semaphore_signal(barrier, inc=1, device_id=device, device_id_type=MESH)

    def await_sent(ref, sem):
        remote(ref, ref, sem, sem, (me, my)).wait_send()

    def await_got(ref, sem):
        remote(ref, ref, sem, sem, (me, my)).wait_recv()

    def tell(step, peers):
        for peer in peers:
            pl.semaphore_signal(
                word.at[step], inc=1, device_id=(peer, my), device_id_type=MESH
            )

    def hear(step, count):
        pl.semaphore_wait(word.at[step], count)

    load_d.wait()
    pl.semaphore_wait(barrier, len(near))

    half, quarter = ql // 2, ql // 4

    def row_copy(part, slot, src):
        first, count, peer = (
            (0, half, far),
            (0, ql, right),
            (half, quarter, left),
            (half + quarter, quarter, left),
            (0, half, left),
            (half, quarter, left),
            (half + quarter, quarter, left),
        )[slot]
        at = pl.ds((1 - part) * ql + first, count)
        slot = part * 7 + slot
        return remote(
            rows.at[src, at], rows.at[src, at], ag_s, ag_r.at[slot], (me, peer)
        )

    def rows_start(part):
        for slot in (0, 2, 1, 3, 4):
            row_copy(part, slot, my).start()

    def rows_relay(part):
        for slot in (2, 3):
            row_copy(part, slot, right).wait_recv()
            row_copy(part, slot + 3, right).start()

    def rows_right(part):
        row_copy(part, 4, right).wait_recv()
        return product_of(part, right)

    def rows_left(part):
        row_copy(part, 1, left).wait_recv()
        return product_of(part, left)

    def rows_far(part):
        for slot in (0, 5, 6):
            row_copy(part, slot, far).wait_recv()
        return product_of(part, far)

    def product_of(part, src):
        at = (1 - part) * ql
        return jnp.dot(
            rows[src, at : at + ql, :], head[row_block(src), :], preferred_element_type=F32
        )

    along = (
        (g, lambda j: x * group + j, lambda j: j * group + g, x),
        (x * 2 + core, lambda j: (j // 2) * group + z * 2 + j % 2,
         lambda j: x * group + j * 2 + core, z),
    )

    def turned(axis, j):
        if axis == 0:
            return rows_t.at[:, j // 2, j % 2, pl.ds(0, hrows), :]
        return rows_t.at[j // 2, :, j % 2, pl.ds(hrows, hrows), :]

    def turn_copy(axis, to, src):
        return remote(
            turned(axis, to),
            rt_buf.at[axis, :, :, pl.ds(pl.multiple_of(src * slots, slots), slots)],
            rt_s,
            rt_r,
            (along[axis][1](to), my),
        )

    def turn_start():
        for m in range(n_mp):
            rows_t[m] = rows[m].T.reshape(n_mp, 2, 2 * hrows, slots)
        for axis in range(2):
            own = along[axis][0]
            for k in range(1, group):
                turn_copy(axis, (own + k) % group, own).start()
            at = pl.ds(pl.multiple_of(own * slots, slots), slots)
            rt_buf[axis, :, :, at] = turned(axis, own)[...]

    rt_others = rt_buf.at[:, :, :, pl.ds(0, (group - 1) * slots)]

    phase("rows_d")
    rows_start(0)
    tell(0, x_near)
    load_h[0].wait()
    acc = product_of(0, my)
    load_send.wait()
    pick = jnp.where(
        lax.broadcasted_iota(jnp.int32, (ql, slots), 0) == send_ref[...], 1.0, 0.0
    ).astype(BF16)

    for copy in load_h[1:]:
        copy.wait()
    hear(0, 2)
    tell(1, z_near)
    phase("relay_d")
    rows_relay(0)
    load_q.wait()
    rows_start(1)
    hear(1, 2)
    tell(2, z_near)
    phase("right_d")
    acc = acc + rows_right(0)
    hear(2, 2)
    tell(3, (partner,))
    phase("left_d")
    acc = acc + rows_left(0)
    phase("far_d")
    acc = acc + rows_far(0)
    hear(3, 1)
    phase("pick")
    dp = acc.astype(BF16)

    picked = contract(pick, dp, 0, 0).astype(BF16)
    out_buf[...] = picked.reshape(n_dp, block, cols)

    phase("fetch")
    def fetch_send(k, carry):
        peer = (me + k) % n_dp
        remote(out_buf.at[peer], fetched.at[me], fe_s, fe_r, (peer, my)).start()
        return carry

    lax.fori_loop(1, n_dp, fetch_send, 0)
    fetched[me] = out_buf[me]

    phase("relay_q")
    rows_relay(1)
    phase("count")
    load_loss.wait()
    load_scale.wait()
    weight = loss_ref[...].T
    load_short.wait()
    short = short_ref[...]
    lane = lax.broadcasted_iota(jnp.int32, (ql, slots), 1)

    count = jnp.zeros((ql, slots), F32)
    for k in range(slots):
        count = count + jnp.where((short if k == 0 else pltpu.roll(short, k, 1)) == lane, 1.0, 0.0)
    phase("rows_q")
    acc = product_of(1, my) + rows_right(1) + rows_left(1) + rows_far(1)
    qp = acc.astype(BF16)

    phase("mask")
    col = lax.broadcasted_iota(jnp.int32, (1, cols), 1)
    seg_col = [
        jnp.where((col >= bounds[s]) & (col < bounds[s + 1]), 1.0, 0.0) for s in range(LOCAL)
    ]
    q_seg = jnp.concatenate([qp * m.astype(BF16) for m in seg_col], axis=0)
    product = qp.astype(F32) * dp.astype(F32)
    pos_prefix = [
        jnp.sum(
            product * jnp.where(col < bounds[s + 1], 1.0, 0.0), axis=1, keepdims=True
        )
        for s in range(LOCAL)
    ]

    phase("fetch_wait")
    await_got(fetched.at[pl.ds(0, n_dp - 1)], fe_r)
    phase("turn")
    turn_start()
    phase("score")
    docs = fetched[...].reshape(slots, cols)
    pieces = contract(q_seg, docs, 1, 1)
    scores = []
    for s in range(LOCAL):
        piece = pieces[s * ql : (s + 1) * ql]
        scores.append(piece if s == 0 else scores[-1] + piece)

    diag = lax.broadcasted_iota(jnp.int32, (ql, slots), 0) == lane
    pos_row = jnp.sum(
        jnp.where(diag, jnp.broadcast_to(pos_prefix[-1], (ql, slots)), 0.0), axis=0, keepdims=True
    )
    score_buf[my, 0:ql, :] = scores[-1]
    score_buf[my, ql : ql + 8, :] = jnp.broadcast_to(pos_row, (8, slots))
    for peer in (far, right, left):
        remote(score_buf.at[my], score_buf.at[my], sc_s, sc_r, (me, peer)).start()

    phase("narrow")
    def width(w, score, pos):
        scale = scale_ref[w] * (1.0 / math.sqrt(bounds[w + 1]))
        return softmax_terms(score, pos, count, scale, weight[:, w : w + 1])

    narrow = [width(w, scores[w], pos_prefix[w]) for w in range(LOCAL)]
    doc_seg = [docs * m.astype(BF16) for m in seg_col]
    wide_at = 256
    docs_low = jnp.concatenate([m[:, :wide_at] for m in doc_seg[:4]], axis=0)
    docs_high = jnp.concatenate([m[:, wide_at:] for m in doc_seg[3:]], axis=0)

    phase("score_wait")
    await_got(score_buf.at[pl.ds(0, n_mp - 1)], sc_r)
    phase("wide")
    parts = [score_buf[m, 0:ql, :] for m in range(n_mp)]
    pos_parts = [
        jnp.sum(
            jnp.where(diag, jnp.concatenate([score_buf[m, ql : ql + 8, :]] * 8, axis=0), 0.0),
            axis=1,
            keepdims=True,
        )
        for m in range(n_mp)
    ]
    score5, pos5 = parts[0] + parts[1], pos_parts[0] + pos_parts[1]
    neg5, posg5 = width(5, score5, pos5)
    neg6, posg6 = width(6, score5 + (parts[2] + parts[3]), pos5 + (pos_parts[2] + pos_parts[3]))
    run_neg = neg6 + jnp.where(my <= 1, neg5, 0.0)
    run_pos = posg6 + jnp.where(my <= 1, posg5, 0.0)
    coeff = [None] * LOCAL
    pos_cols = jnp.zeros((ql, cols), F32)
    for s in reversed(range(LOCAL)):
        run_neg = run_neg + jnp.where(my == 0, narrow[s][0], 0.0)
        run_pos = run_pos + jnp.where(my == 0, narrow[s][1], 0.0)
        coeff[s] = run_neg.astype(BF16)
        pos_cols = pos_cols + run_pos * seg_col[s]

    phase("by_slot")
    by_slot = jnp.concatenate(
        [
            contract(jnp.concatenate(coeff[:4], axis=0), q_seg[: 4 * ql, :wide_at], 0, 0),
            contract(jnp.concatenate(coeff[3:], axis=0), q_seg[3 * ql :, wide_at:], 0, 0),
        ],
        axis=1,
    ).astype(BF16)
    back_buf[...] = by_slot.reshape(n_dp, block, cols)

    def back_send(k, carry):
        peer = (me + k) % n_dp
        remote(back_buf.at[peer], returned.at[me], ba_s, ba_r, (peer, my)).start()
        return carry

    lax.fori_loop(1, n_dp, back_send, 0)
    returned[me] = back_buf[me]

    phase("grad_q")
    query_back = jnp.concatenate(
        [
            jnp.dot(jnp.concatenate(coeff[:4], axis=1), docs_low, preferred_element_type=F32),
            jnp.dot(jnp.concatenate(coeff[3:], axis=1), docs_high, preferred_element_type=F32),
        ],
        axis=1,
    )
    grad_q = (query_back + pos_cols * dp.astype(F32)).astype(BF16)

    def gr_at(axis, part, slot):
        if slot in (0, 3, 5, 7):
            return gp_r
        return gr_r.at[axis, slot - 8 if part == 0 else 5 + slot // 2]

    def grad_copy(axis, part, slot, src, peer, first=0, count=ql):
        at = pl.ds(pl.multiple_of(src * slots + part * ql + first, half), count)
        return remote(
            grads.at[axis, at], grads.at[axis, at],
            gr_s, gr_at(axis, part, slot), (peer, my),
        )

    def grad_send(*args):
        grad_copy(*args).start()

    def keep(part, grad):
        for axis in range(2):
            at = pl.ds(pl.multiple_of(along[axis][0] * slots + part * ql, ql), ql)
            grads[axis, at, :] = grad

    def spread_d(grad):
        keep(1, grad)
        for k in (4, 2, 6, 0):
            for axis in range(2):
                own, device, _, _ = along[axis]
                peer = partner if k == 0 else device((own + k) % group)
                grad_send(axis, 1, k, own, peer)

    def spread_q(grad):
        keep(0, grad)
        for axis in range(2):
            own, device, _, _ = along[axis]
            up, down = device((own + 2) % group), device((own + 6) % group)
            grad_send(axis, 0, 8, own, up, 0, half)
            grad_send(axis, 0, 9, own, down, half, half)
            grad_send(axis, 0, 10, own, up, half, half)
            grad_send(axis, 0, 11, own, down, 0, half)
            grad_send(axis, 0, 0, own, partner)

    def relay_q():
        for axis in range(2):
            own, device, _, _ = along[axis]
            up, down = (own + 2) % group, (own + 6) % group
            grad_copy(axis, 0, 8, down, me, 0, half).wait_recv()
            grad_send(axis, 0, 12, down, device(up), 0, half)
            grad_copy(axis, 0, 9, up, me, half, half).wait_recv()
            grad_send(axis, 0, 13, up, device(down), half, half)

    def forward_q():
        for axis in range(2):
            own = along[axis][0]
            up, down, beyond = (own + 2) % group, (own + 6) % group, (own + 4) % group
            grad_copy(axis, 0, 10, down, me, half, half).wait_recv()
            grad_send(axis, 0, 3, down, partner)
            grad_copy(axis, 0, 11, up, me, 0, half).wait_recv()
            grad_send(axis, 0, 7, up, partner)
        for axis in range(2):
            beyond = (along[axis][0] + 4) % group
            grad_copy(axis, 0, 12, beyond, me, 0, half).wait_recv()
            grad_copy(axis, 0, 13, beyond, me, half, half).wait_recv()
            grad_send(axis, 0, 5, beyond, partner)

    def forward_d():
        for k in (2, 6, 4):
            for axis in range(2):
                src = (along[axis][0] + group - k) % group
                grad_copy(axis, 1, k, src, me).wait_recv()
                grad_send(axis, 1, k + 1, src, partner)

    def share(grad, part, got, send_sem, recv_sem):
        for k in (2, 1, 3):
            peer = (my + k) % n_mp
            part[k] = contract(grad, head[row_block(peer), :], 1, 1).astype(BF16)
            remote(part.at[k], got.at[k], send_sem, recv_sem, (me, peer)).start()
        return contract(grad, head[row_block(my), :], 1, 1)

    def gather_parts(own, got):
        for k in (1, 3, 2):
            own = own + got[k].astype(F32)
        return own

    phase("spread_q")
    spread_q(grad_q)
    phase("share_q")
    own_q = share(grad_q, part_q, got_q, pq_s, pq_r)

    phase("relay_gq")
    relay_q()
    phase("back_wait")
    await_got(returned.at[pl.ds(0, n_dp - 1)], ba_r)
    phase("grad_d")
    doc_back = jnp.dot(pick, returned[...].reshape(slots, cols), preferred_element_type=F32)
    grad_d = (pos_cols * qp.astype(F32) + doc_back).astype(BF16)
    spread_d(grad_d)
    phase("share_d")
    own_d = share(grad_d, part_d, got_d, pd_s, pd_r)
    phase("forward_q")
    forward_q()
    phase("forward_d")
    forward_d()
    phase("rt_wait")
    await_got(rt_others, rt_r)
    phase("settle")
    await_got(grads.at[0], gp_r)
    phase("head")
    own_h = []
    for axis in range(2):
        mine = along[axis][3]
        total = jnp.dot(
            rt_buf[axis].reshape(n_mp * hrows, group * slots), grads[axis],
            preferred_element_type=F32,
        )
        full_h[axis] = total.reshape(n_mp, hrows, cols)
        part_h[axis] = full_h[axis].astype(BF16)
        for k in (2, 1, 3):
            peer = (mine + k) % n_mp
            remote(
                part_h.at[axis, peer], got_h.at[axis, k], hg_s, hg_r, (along[axis][2](peer), my)
            ).start()
        own_h.append(full_h[axis, mine])
    phase("query_out")
    await_got(got_q.at[pl.ds(1, n_mp - 1)], pq_r)
    qg_ref[...] = gather_parts(own_q, got_q).astype(BF16)

    save_q = pltpu.make_async_copy(qg_ref, qg_hbm, load_sem.at[10])
    save_q.start()
    phase("doc_out")
    await_got(got_d.at[pl.ds(1, n_mp - 1)], pd_r)
    dg_ref[...] = gather_parts(own_d, got_d).astype(BF16)
    save_d = pltpu.make_async_copy(dg_ref, dg_hbm, load_sem.at[11])
    save_d.start()
    phase("head_out")
    await_got(got_h.at[:, pl.ds(1, n_mp - 1)], hg_r)
    for axis in range(2):
        hg_ref[axis * hrows : (axis + 1) * hrows, :] = gather_parts(own_h[axis], got_h.at[axis])
    phase("drain")
    save_h = pltpu.make_async_copy(hg_ref, hg_hbm, load_sem.at[12])
    save_h.start()
    await_sent(rows.at[pl.ds(0, 3)], ag_s)
    await_sent(out_buf.at[pl.ds(0, n_dp - 1)], fe_s)
    await_sent(rt_others, rt_s)
    await_sent(score_buf.at[pl.ds(0, n_mp - 1)], sc_s)
    await_sent(back_buf.at[pl.ds(0, n_dp - 1)], ba_s)
    await_sent(grads.at[:, pl.ds(0, 896)], gr_s)
    await_sent(part_q.at[pl.ds(1, n_mp - 1)], pq_s)
    await_sent(part_d.at[pl.ds(1, n_mp - 1)], pd_s)
    await_sent(part_h.at[:, pl.ds(1, n_mp - 1)], hg_s)
    phase("saved")
    for copy in (save_q, save_d, save_h):
        copy.wait()
    phase(None)


def hand_out(a, b, c, out_a, out_b, out_c, sem):
    copies = [
        pltpu.make_async_copy(src, dst, sem.at[i])
        for i, (src, dst) in enumerate(((c, out_c), (a, out_a), (b, out_b)))
    ]
    for copy in copies:
        copy.start()
    for copy in copies:
        copy.wait()


def on_device(query_rows, doc_rows, head, logit_scale, loss_grad, shortlist, send_rows):
    ql, cols = query_rows.shape
    dma = pltpu.SemaphoreType.DMA
    one = dma(())
    hbm = pl.BlockSpec(memory_space=pltpu.HBM)
    operands = (logit_scale, loss_grad.T, shortlist, send_rows, query_rows, doc_rows, head)
    shapes = (
        jax.ShapeDtypeStruct((ql, cols), BF16),
        jax.ShapeDtypeStruct((ql, cols), BF16),
        jax.ShapeDtypeStruct((80, cols), F32),
    )
    results = pl.pallas_call(
        kernel,
        out_shape=shapes,
        in_specs=[hbm] * 7,
        out_specs=(hbm, hbm, hbm),
        scratch_shapes=[
            pltpu.VMEM((ql, cols), BF16),
            pltpu.VMEM((ql, cols), BF16),
            pltpu.VMEM((80, cols), F32),
            pltpu.SMEM((NW,), F32),
            pltpu.VMEM((NW, ql), F32),
            pltpu.VMEM((ql, 128), jnp.int32),
            pltpu.VMEM((1, 128), jnp.int32),
            pltpu.VMEM((4, 2 * ql, cols), BF16),
            pltpu.VMEM((4 * cols, cols), BF16),
            pltpu.VMEM((4, 4, 2, 80, 128), BF16),
            pltpu.VMEM((2, 4, 40, 1024), BF16),
            pltpu.VMEM((2, 1024, cols), BF16),
            pltpu.VMEM((32, 4, cols), BF16),
            pltpu.VMEM((32, 4, cols), BF16),
            pltpu.VMEM((32, 4, cols), BF16),
            pltpu.VMEM((32, 4, cols), BF16),
            pltpu.VMEM((4, ql + 8, 128), F32),
            pltpu.VMEM((4, ql, cols), BF16),
            pltpu.VMEM((4, ql, cols), BF16),
            pltpu.VMEM((4, ql, cols), BF16),
            pltpu.VMEM((4, ql, cols), BF16),
            pltpu.VMEM((2, 4, 40, cols), F32),
            pltpu.VMEM((2, 4, 40, cols), BF16),
            pltpu.VMEM((2, 4, 40, cols), BF16),
            dma((13,)), one, dma((14,)), one, one, one, one, one, one, one, one,
            one, dma((2, 9)), one, one, one, one, one, one, one,
            pltpu.SemaphoreType.REGULAR((4,)),
        ],
        compiler_params=pltpu.CompilerParams(
            collective_id=0, has_side_effects=True, vmem_limit_bytes=48 * 1024 * 1024
        ),
    )(*[pltpu.with_memory_space_constraint(a, pltpu.HBM) for a in operands])
    anywhere = pl.BlockSpec(memory_space=pl.ANY)
    return pl.pallas_call(
        hand_out,
        out_shape=shapes,
        in_specs=[anywhere] * 3,
        out_specs=(anywhere,) * 3,
        scratch_shapes=[dma((3,))],
        compiler_params=pltpu.CompilerParams(vmem_limit_bytes=1024 * 1024),
    )(*results)


def solution(mesh):
    placed = (
        P("dp", "mp"),
        P("dp", "mp"),
        P(None, "mp"),
        P(),
        P("dp", None),
        P("dp", None),
        P("dp", None),
    )
    return jax.shard_map(
        on_device,
        mesh=mesh,
        in_specs=placed,
        out_specs=(P("dp", "mp"), P("dp", "mp"), P("dp", "mp")),
        check_vma=False,
    )
```

time: 53 us -> 48.1 us (0.908)
  Pallas kernels: 50.3 us -> 47.4 us
  local copies, waits for them, and re-layouts: 1.95 us -> 0 us
    pallas_call x1 -> x2, Pallas kernels: 50.3 us -> 47.4 us  [the longest x1 46.6 us: on_device(): pl.pallas_call(kernel, out_shape=shapes, in_specs=[hbm] * 7, out_specs=(h...]
    unnamed x3 -> x0, local copies, waits for them, and re-layouts: 1.95 us -> none
where the time goes in v3:
time: 48.1 us; the launch traced here: 48 us
  Pallas kernels  47.4 us (99%)
  between operations  0.64 us (1%)
    pallas_call x1, Pallas kernels, on_device(): pl.pallas_call(kernel, out_shape=shapes, in_specs=[hbm] * 7, out_specs=(h...  46.6 us

profile of v3, /device:TPU:1, one launch (start us, length us, event | category | flops | bytes accessed | tf_op | source)
XLA Modules:
  0.0 48.0 jit_solution(10978980568912770687)
XLA Ops:
  0.6 46.6 %shard_map.94 = (bf16[64,640]{1,0:T(8,128)(2,1)S(1)}, bf16[64,640]{1,0:T(8,128)(2,1)S(1)}, f32[80,640]{1,0:T(8,128)S(1)}) custom-call(f32[7]{0:T(128)} %scale_hbm.1, f32[7,64]{1,0:T(8,128)} %bitcast.1, s32[64,128]{1,0:T(8,128)} %short_hbm.1, s32[1,128]{1,0:T(1,128)} %send_hbm.1, bf16[64,640]{1,0:T(8,128)(2,1)} %q_hbm.1, bf16[64,640]{1,0:T(8,128)(2,1)} %d_hbm.1, ...), custom_call_target="tpu_custom_call" | custom-call | tf_op jit(solution)/shard_map/pallas_call | solution.py:550
  47.3 0.8 %shard_map.95 = (bf16[64,640]{1,0:T(8,128)(2,1)}, bf16[64,640]{1,0:T(8,128)(2,1)}, f32[80,640]{1,0:T(8,128)}) custom-call(bf16[64,640]{1,0:T(8,128)(2,1)S(1)} %get-tuple-element.6.a, bf16[64,640]{1,0:T(8,128)(2,1)S(1)} %get-tuple-element.7.b, f32[80,640]{1,0:T(8,128)S(1)} %get-tuple-element.8.c), custom_call_target="tpu_custom_call" | custom-call | tf_op jit(solution)/shard_map/pallas_call | solution.py:589

commit v4 on v3

--- a/solution.py
+++ b/solution.py
@@ -55,11 +55,11 @@
 
 def kernel(
     scale_hbm, loss_hbm, short_hbm, send_hbm, q_hbm, d_hbm, head_hbm,
-    qg_hbm, dg_hbm, hg_hbm,
     qg_ref, dg_ref, hg_ref,
-    scale_ref, loss_ref, short_ref, send_ref, rows, head, rows_t, rt_buf, grads,
+    scale_ref, loss_ref, short_ref, send_ref, rows, head, rows_t, rt_buf, grads_0, grads_1,
     out_buf, fetched, back_buf, returned,
-    score_buf, part_q, got_q, part_d, got_d, full_h, part_h, got_h,
+    score_buf, part_q, got_q, part_d, got_d,
+    full_0, full_1, part_0, part_1, got_0, got_1,
     load_sem, ag_s, ag_r, fe_s, fe_r, sc_s, sc_r, rt_s, rt_r, ba_s, ba_r,
     gr_s, gr_r, gp_r, pq_s, pq_r, pd_s, pd_r, hg_s, hg_r, word,
 ):
@@ -67,7 +67,11 @@
     group = 8
     slots = 128
     block = 4
-    hrows = 40
+    hrows = 80
+    cuts = (0, 384, cols)
+    grads, full_h, part_h, got_h = (
+        (grads_0, grads_1), (full_0, full_1), (part_0, part_1), (got_0, got_1)
+    )
     me = lax.axis_index("dp")
     my = lax.axis_index("mp")
     x = me // group
@@ -122,6 +126,14 @@
     def await_got(ref, sem):
         remote(ref, ref, sem, sem, (me, my)).wait_recv()
 
+    steps = [(i, j, k) for i in (2, 1, 3, 0) for j in (2, 1, 3, 0) for k in (0, 1)]
+    steps.sort(key=lambda d: -(min(d[0], 4 - d[0]) + min(d[1], 4 - d[1])))
+    others = [
+        ((x + i) % 4 * group + (z + j) % 4 * 2 + (core if k == 0 else 1 - core))
+        for i, j, k in steps
+        if (i, j, k) != (0, 0, 0)
+    ]
+
     def tell(step, peers):
         for peer in peers:
             pl.semaphore_signal(
@@ -188,8 +200,8 @@
 
     def turned(axis, j):
         if axis == 0:
-            return rows_t.at[:, j // 2, j % 2, pl.ds(0, hrows), :]
-        return rows_t.at[j // 2, :, j % 2, pl.ds(hrows, hrows), :]
+            return rows_t.at[:, j // 2, j % 2]
+        return rows_t.at[j // 2, :, j % 2]
 
     def turn_copy(axis, to, src):
         return remote(
@@ -200,10 +212,12 @@
             (along[axis][1](to), my),
         )
 
-    def turn_start():
+    def turn_rows():
         for m in range(n_mp):
-            rows_t[m] = rows[m].T.reshape(n_mp, 2, 2 * hrows, slots)
-        for axis in range(2):
+            rows_t[m] = rows[m].T.reshape(n_mp, 2, hrows, slots)
+
+    def turn_start(axes):
+        for axis in axes:
             own = along[axis][0]
             for k in range(1, group):
                 turn_copy(axis, (own + k) % group, own).start()
@@ -248,12 +262,8 @@
     out_buf[...] = picked.reshape(n_dp, block, cols)
 
     phase("fetch")
-    def fetch_send(k, carry):
-        peer = (me + k) % n_dp
+    for peer in others:
         remote(out_buf.at[peer], fetched.at[me], fe_s, fe_r, (peer, my)).start()
-        return carry
-
-    lax.fori_loop(1, n_dp, fetch_send, 0)
     fetched[me] = out_buf[me]
 
     phase("relay_q")
@@ -273,6 +283,9 @@
     acc = product_of(1, my) + rows_right(1) + rows_left(1) + rows_far(1)
     qp = acc.astype(BF16)
 
+    phase("turn0")
+    turn_rows()
+    turn_start((0,))
     phase("mask")
     col = lax.broadcasted_iota(jnp.int32, (1, cols), 1)
     seg_col = [
@@ -290,7 +303,7 @@
     phase("fetch_wait")
     await_got(fetched.at[pl.ds(0, n_dp - 1)], fe_r)
     phase("turn")
-    turn_start()
+    turn_start((1,))
     phase("score")
     docs = fetched[...].reshape(slots, cols)
     pieces = contract(q_seg, docs, 1, 1)
@@ -354,12 +367,8 @@
     ).astype(BF16)
     back_buf[...] = by_slot.reshape(n_dp, block, cols)
 
-    def back_send(k, carry):
-        peer = (me + k) % n_dp
+    for peer in others:
         remote(back_buf.at[peer], returned.at[me], ba_s, ba_r, (peer, my)).start()
-        return carry
-
-    lax.fori_loop(1, n_dp, back_send, 0)
     returned[me] = back_buf[me]
 
     phase("grad_q")
@@ -374,14 +383,14 @@
 
     def gr_at(axis, part, slot):
         if slot in (0, 3, 5, 7):
-            return gp_r
-        return gr_r.at[axis, slot - 8 if part == 0 else 5 + slot // 2]
-
-    def grad_copy(axis, part, slot, src, peer, first=0, count=ql):
-        at = pl.ds(pl.multiple_of(src * slots + part * ql + first, half), count)
+            return gp_r.at[slot // 2]
+        return gr_r.at[axis, part, slot // 2 - 1]
+
+    def grad_copy(axis, part, slot, src, peer):
+        at = pl.ds(pl.multiple_of(src * slots + part * ql, ql), ql)
         return remote(
-            grads.at[axis, at], grads.at[axis, at],
-            gr_s, gr_at(axis, part, slot), (peer, my),
+            grads[axis].at[at], grads[axis].at[at],
+            gr_s.at[axis], gr_at(axis, part, slot), (peer, my),
         )
 
     def grad_send(*args):
@@ -390,56 +399,20 @@
     def keep(part, grad):
         for axis in range(2):
             at = pl.ds(pl.multiple_of(along[axis][0] * slots + part * ql, ql), ql)
-            grads[axis, at, :] = grad
-
-    def spread_d(grad):
-        keep(1, grad)
+            grads[axis][at, :] = grad[:, cuts[axis] : cuts[axis + 1]]
+
+    def spread(part, grad):
+        keep(part, grad)
         for k in (4, 2, 6, 0):
             for axis in range(2):
                 own, device, _, _ = along[axis]
-                peer = partner if k == 0 else device((own + k) % group)
-                grad_send(axis, 1, k, own, peer)
-
-    def spread_q(grad):
-        keep(0, grad)
+                grad_send(axis, part, k, own, partner if k == 0 else device((own + k) % group))
+
+    def forward(part, k):
         for axis in range(2):
-            own, device, _, _ = along[axis]
-            up, down = device((own + 2) % group), device((own + 6) % group)
-            grad_send(axis, 0, 8, own, up, 0, half)
-            grad_send(axis, 0, 9, own, down, half, half)
-            grad_send(axis, 0, 10, own, up, half, half)
-            grad_send(axis, 0, 11, own, down, 0, half)
-            grad_send(axis, 0, 0, own, partner)
-
-    def relay_q():
-        for axis in range(2):
-            own, device, _, _ = along[axis]
-            up, down = (own + 2) % group, (own + 6) % group
-            grad_copy(axis, 0, 8, down, me, 0, half).wait_recv()
-            grad_send(axis, 0, 12, down, device(up), 0, half)
-            grad_copy(axis, 0, 9, up, me, half, half).wait_recv()
-            grad_send(axis, 0, 13, up, device(down), half, half)
-
-    def forward_q():
-        for axis in range(2):
-            own = along[axis][0]
-            up, down, beyond = (own + 2) % group, (own + 6) % group, (own + 4) % group
-            grad_copy(axis, 0, 10, down, me, half, half).wait_recv()
-            grad_send(axis, 0, 3, down, partner)
-            grad_copy(axis, 0, 11, up, me, 0, half).wait_recv()
-            grad_send(axis, 0, 7, up, partner)
-        for axis in range(2):
-            beyond = (along[axis][0] + 4) % group
-            grad_copy(axis, 0, 12, beyond, me, 0, half).wait_recv()
-            grad_copy(axis, 0, 13, beyond, me, half, half).wait_recv()
-            grad_send(axis, 0, 5, beyond, partner)
-
-    def forward_d():
-        for k in (2, 6, 4):
-            for axis in range(2):
-                src = (along[axis][0] + group - k) % group
-                grad_copy(axis, 1, k, src, me).wait_recv()
-                grad_send(axis, 1, k + 1, src, partner)
+            src = (along[axis][0] + group - k) % group
+            grad_copy(axis, part, k, src, me).wait_recv()
+            grad_send(axis, part, k + 1, src, partner)
 
     def share(grad, part, got, send_sem, recv_sem):
         for k in (2, 1, 3):
@@ -453,75 +426,86 @@
             own = own + got[k].astype(F32)
         return own
 
-    phase("spread_q")
-    spread_q(grad_q)
     phase("share_q")
     own_q = share(grad_q, part_q, got_q, pq_s, pq_r)
 
-    phase("relay_gq")
-    relay_q()
+    phase("spread_q")
+    spread(0, grad_q)
     phase("back_wait")
     await_got(returned.at[pl.ds(0, n_dp - 1)], ba_r)
     phase("grad_d")
     doc_back = jnp.dot(pick, returned[...].reshape(slots, cols), preferred_element_type=F32)
     grad_d = (pos_cols * qp.astype(F32) + doc_back).astype(BF16)
-    spread_d(grad_d)
+    spread(1, grad_d)
     phase("share_d")
     own_d = share(grad_d, part_d, got_d, pd_s, pd_r)
     phase("forward_q")
-    forward_q()
+    for k in (2, 6, 4):
+        forward(0, k)
+    await_got(rt_others, rt_r)
+    chips = (z, x)
+    total_h = [None, None]
+
+    def chip_product(axis, k):
+        at = pl.ds(pl.multiple_of((chips[axis] + 4 - k // 2) % 4 * 2 * slots, slots), 2 * slots)
+        term = jnp.dot(
+            rt_buf[axis, :, :, at].reshape(n_mp * hrows, 2 * slots), grads[axis][at, :],
+            preferred_element_type=F32,
+        )
+        return term if total_h[axis] is None else total_h[axis] + term
+
+    def chip_arrived(k):
+        await_got(rows.at[0], gp_r.at[(k + 1) // 2 if k else 0])
+
+    phase("own_h")
+    chip_arrived(0)
+    for axis in range(2):
+        total_h[axis] = chip_product(axis, 0)
     phase("forward_d")
-    forward_d()
-    phase("rt_wait")
-    await_got(rt_others, rt_r)
+    for k in (2, 6, 4):
+        forward(1, k)
+    for k in (2, 6):
+        phase("near_h")
+        chip_arrived(k)
+        for axis in range(2):
+            total_h[axis] = chip_product(axis, k)
     phase("settle")
-    await_got(grads.at[0], gp_r)
+    chip_arrived(4)
     phase("head")
     own_h = []
     for axis in range(2):
         mine = along[axis][3]
-        total = jnp.dot(
-            rt_buf[axis].reshape(n_mp * hrows, group * slots), grads[axis],
-            preferred_element_type=F32,
-        )
-        full_h[axis] = total.reshape(n_mp, hrows, cols)
-        part_h[axis] = full_h[axis].astype(BF16)
+        full_h[axis][...] = chip_product(axis, 4).reshape(n_mp, hrows, -1)
+        part_h[axis][...] = full_h[axis][...].astype(BF16)
         for k in (2, 1, 3):
             peer = (mine + k) % n_mp
             remote(
-                part_h.at[axis, peer], got_h.at[axis, k], hg_s, hg_r, (along[axis][2](peer), my)
+                part_h[axis].at[peer], got_h[axis].at[k], hg_s.at[axis], hg_r.at[axis],
+                (along[axis][2](peer), my),
             ).start()
-        own_h.append(full_h[axis, mine])
+        own_h.append(full_h[axis][mine])
     phase("query_out")
     await_got(got_q.at[pl.ds(1, n_mp - 1)], pq_r)
     qg_ref[...] = gather_parts(own_q, got_q).astype(BF16)
 
-    save_q = pltpu.make_async_copy(qg_ref, qg_hbm, load_sem.at[10])
-    save_q.start()
     phase("doc_out")
     await_got(got_d.at[pl.ds(1, n_mp - 1)], pd_r)
     dg_ref[...] = gather_parts(own_d, got_d).astype(BF16)
-    save_d = pltpu.make_async_copy(dg_ref, dg_hbm, load_sem.at[11])
-    save_d.start()
     phase("head_out")
-    await_got(got_h.at[:, pl.ds(1, n_mp - 1)], hg_r)
     for axis in range(2):
-        hg_ref[axis * hrows : (axis + 1) * hrows, :] = gather_parts(own_h[axis], got_h.at[axis])
+        await_got(got_h[axis].at[pl.ds(1, n_mp - 1)], hg_r.at[axis])
+        hg_ref[:, cuts[axis] : cuts[axis + 1]] = gather_parts(own_h[axis], got_h[axis])
     phase("drain")
-    save_h = pltpu.make_async_copy(hg_ref, hg_hbm, load_sem.at[12])
-    save_h.start()
     await_sent(rows.at[pl.ds(0, 3)], ag_s)
     await_sent(out_buf.at[pl.ds(0, n_dp - 1)], fe_s)
     await_sent(rt_others, rt_s)
     await_sent(score_buf.at[pl.ds(0, n_mp - 1)], sc_s)
     await_sent(back_buf.at[pl.ds(0, n_dp - 1)], ba_s)
-    await_sent(grads.at[:, pl.ds(0, 896)], gr_s)
+    for axis in range(2):
+        await_sent(grads[axis].at[pl.ds(0, 896)], gr_s.at[axis])
+        await_sent(part_h[axis].at[pl.ds(1, n_mp - 1)], hg_s.at[axis])
     await_sent(part_q.at[pl.ds(1, n_mp - 1)], pq_s)
     await_sent(part_d.at[pl.ds(1, n_mp - 1)], pd_s)
-    await_sent(part_h.at[:, pl.ds(1, n_mp - 1)], hg_s)
-    phase("saved")
-    for copy in (save_q, save_d, save_h):
-        copy.wait()
     phase(None)
 
 
@@ -541,6 +525,7 @@
     dma = pltpu.SemaphoreType.DMA
     one = dma(())
     hbm = pl.BlockSpec(memory_space=pltpu.HBM)
+    vmem = pl.BlockSpec(memory_space=pltpu.VMEM)
     operands = (logit_scale, loss_grad.T, shortlist, send_rows, query_rows, doc_rows, head)
     shapes = (
         jax.ShapeDtypeStruct((ql, cols), BF16),
@@ -551,11 +536,8 @@
         kernel,
         out_shape=shapes,
         in_specs=[hbm] * 7,
-        out_specs=(hbm, hbm, hbm),
+        out_specs=(vmem, vmem, vmem),
         scratch_shapes=[
-            pltpu.VMEM((ql, cols), BF16),
-            pltpu.VMEM((ql, cols), BF16),
-            pltpu.VMEM((80, cols), F32),
             pltpu.SMEM((NW,), F32),
             pltpu.VMEM((NW, ql), F32),
             pltpu.VMEM((ql, 128), jnp.int32),
@@ -563,8 +545,9 @@
             pltpu.VMEM((4, 2 * ql, cols), BF16),
             pltpu.VMEM((4 * cols, cols), BF16),
             pltpu.VMEM((4, 4, 2, 80, 128), BF16),
-            pltpu.VMEM((2, 4, 40, 1024), BF16),
-            pltpu.VMEM((2, 1024, cols), BF16),
+            pltpu.VMEM((2, 4, 80, 1024), BF16),
+            pltpu.VMEM((1024, 384), BF16),
+            pltpu.VMEM((1024, 256), BF16),
             pltpu.VMEM((32, 4, cols), BF16),
             pltpu.VMEM((32, 4, cols), BF16),
             pltpu.VMEM((32, 4, cols), BF16),
@@ -574,11 +557,14 @@
             pltpu.VMEM((4, ql, cols), BF16),
             pltpu.VMEM((4, ql, cols), BF16),
             pltpu.VMEM((4, ql, cols), BF16),
-            pltpu.VMEM((2, 4, 40, cols), F32),
-            pltpu.VMEM((2, 4, 40, cols), BF16),
-            pltpu.VMEM((2, 4, 40, cols), BF16),
-            dma((13,)), one, dma((14,)), one, one, one, one, one, one, one, one,
-            one, dma((2, 9)), one, one, one, one, one, one, one,
+            pltpu.VMEM((4, 80, 384), F32),
+            pltpu.VMEM((4, 80, 256), F32),
+            pltpu.VMEM((4, 80, 384), BF16),
+            pltpu.VMEM((4, 80, 256), BF16),
+            pltpu.VMEM((4, 80, 384), BF16),
+            pltpu.VMEM((4, 80, 256), BF16),
+            dma((10,)), one, dma((14,)), one, one, one, one, one, one, one, one,
+            dma((2,)), dma((2, 2, 3)), dma((4,)), one, one, one, one, dma((2,)), dma((2,)),
             pltpu.SemaphoreType.REGULAR((4,)),
         ],
         compiler_params=pltpu.CompilerParams(

time: 48.1 us -> 45 us (0.936)
  Pallas kernels: 47.4 us -> 44.3 us
    pallas_call x1, Pallas kernels: 46.6 us -> 43.5 us  [on_device(): pl.pallas_call(kernel, out_shape=shapes, in_specs=[hbm] * 7, out_specs=(v...]
where the time goes in v4:
time: 45 us; the launch traced here: 44.9 us
  Pallas kernels  44.3 us (98%)
  between operations  0.64 us (1%)
    pallas_call x1, Pallas kernels, on_device(): pl.pallas_call(kernel, out_shape=shapes, in_specs=[hbm] * 7, out_specs=(v...  43.5 us

profile of v4, /device:TPU:1, one launch (start us, length us, event | category | flops | bytes accessed | tf_op | source)
XLA Modules:
  0.0 44.9 jit_solution(13823323336740256259)
XLA Ops:
  0.6 43.5 %shard_map.94 = (bf16[64,640]{1,0:T(8,128)(2,1)S(1)}, bf16[64,640]{1,0:T(8,128)(2,1)S(1)}, f32[80,640]{1,0:T(8,128)S(1)}) custom-call(f32[7]{0:T(128)} %scale_hbm.1, f32[7,64]{1,0:T(8,128)} %bitcast.1, s32[64,128]{1,0:T(8,128)} %short_hbm.1, s32[1,128]{1,0:T(1,128)} %send_hbm.1, bf16[64,640]{1,0:T(8,128)(2,1)} %q_hbm.1, bf16[64,640]{1,0:T(8,128)(2,1)} %d_hbm.1, ...), custom_call_target="tpu_custom_call" | custom-call | tf_op jit(solution)/shard_map/pallas_call | solution.py:535
  44.2 0.8 %shard_map.95 = (bf16[64,640]{1,0:T(8,128)(2,1)}, bf16[64,640]{1,0:T(8,128)(2,1)}, f32[80,640]{1,0:T(8,128)}) custom-call(bf16[64,640]{1,0:T(8,128)(2,1)S(1)} %get-tuple-element.6.a, bf16[64,640]{1,0:T(8,128)(2,1)S(1)} %get-tuple-element.7.b, f32[80,640]{1,0:T(8,128)S(1)} %get-tuple-element.8.c), custom_call_target="tpu_custom_call" | custom-call | tf_op jit(solution)/shard_map/pallas_call | solution.py:575

commit v5 on v4

--- a/solution.py
+++ b/solution.py
@@ -61,7 +61,7 @@
     score_buf, part_q, got_q, part_d, got_d,
     full_0, full_1, part_0, part_1, got_0, got_1,
     load_sem, ag_s, ag_r, fe_s, fe_r, sc_s, sc_r, rt_s, rt_r, ba_s, ba_r,
-    gr_s, gr_r, gp_r, pq_s, pq_r, pd_s, pd_r, hg_s, hg_r, word,
+    gr_s, gr_r, pq_s, pq_r, pd_s, pd_r, hg_s, hg_r, word,
 ):
     n_dp, n_mp, ql, cols = 32, 4, 64, 640
     group = 8
@@ -192,25 +192,21 @@
             rows[src, at : at + ql, :], head[row_block(src), :], preferred_element_type=F32
         )
 
-    along = (
-        (g, lambda j: x * group + j, lambda j: j * group + g, x),
-        (x * 2 + core, lambda j: (j // 2) * group + z * 2 + j % 2,
-         lambda j: x * group + j * 2 + core, z),
-    )
-
-    def turned(axis, j):
-        if axis == 0:
-            return rows_t.at[:, j // 2, j % 2]
-        return rows_t.at[j // 2, :, j % 2]
-
-    def turn_copy(axis, to, src):
-        return remote(
-            turned(axis, to),
-            rt_buf.at[axis, :, :, pl.ds(pl.multiple_of(src * slots, slots), slots)],
-            rt_s,
-            rt_r,
-            (along[axis][1](to), my),
-        )
+    home = (1, 0)
+    chips = (z, x)
+    spots = (x, z)
+
+    def gatherer(axis, pos):
+        return x * group + pos * 2 + home[0] if axis == 0 else pos * group + z * 2 + home[1]
+
+    def reducer(axis, pos, c):
+        return pos * group + z * 2 + c if axis == 0 else x * group + pos * 2 + c
+
+    def items(axis):
+        return chips[axis] * 2 + core
+
+    def turned(axis, pos):
+        return rows_t.at[:, pos] if axis == 0 else rows_t.at[pos]
 
     def turn_rows():
         for m in range(n_mp):
@@ -218,11 +214,23 @@
 
     def turn_start(axes):
         for axis in axes:
-            own = along[axis][0]
-            for k in range(1, group):
-                turn_copy(axis, (own + k) % group, own).start()
-            at = pl.ds(pl.multiple_of(own * slots, slots), slots)
-            rt_buf[axis, :, :, at] = turned(axis, own)[...]
+            at = pl.ds(pl.multiple_of(items(axis) * slots, slots), slots)
+            for k in (2, 1, 3):
+                pos = (chips[axis] + k) % n_mp
+                remote(
+                    turned(axis, pos), rt_buf.at[:, :, :, at], rt_s, rt_r,
+                    (gatherer(axis, pos), my),
+                ).start()
+
+            @pl.when(core == home[axis])
+            def _():
+                rt_buf[:, :, :, at] = turned(axis, chips[axis])[...]
+
+            @pl.when(core != home[axis])
+            def _():
+                remote(
+                    turned(axis, chips[axis]), rt_buf.at[:, :, :, at], rt_s, rt_r, (partner, my)
+                ).start()
 
     rt_others = rt_buf.at[:, :, :, pl.ds(0, (group - 1) * slots)]
 
@@ -381,38 +389,22 @@
     )
     grad_q = (query_back + pos_cols * dp.astype(F32)).astype(BF16)
 
-    def gr_at(axis, part, slot):
-        if slot in (0, 3, 5, 7):
-            return gp_r.at[slot // 2]
-        return gr_r.at[axis, part, slot // 2 - 1]
-
-    def grad_copy(axis, part, slot, src, peer):
-        at = pl.ds(pl.multiple_of(src * slots + part * ql, ql), ql)
-        return remote(
-            grads[axis].at[at], grads[axis].at[at],
-            gr_s.at[axis], gr_at(axis, part, slot), (peer, my),
-        )
-
-    def grad_send(*args):
-        grad_copy(*args).start()
-
-    def keep(part, grad):
+    def spread(part, grad):
         for axis in range(2):
-            at = pl.ds(pl.multiple_of(along[axis][0] * slots + part * ql, ql), ql)
+            at = pl.ds(pl.multiple_of(items(axis) * slots + part * ql, ql), ql)
             grads[axis][at, :] = grad[:, cuts[axis] : cuts[axis + 1]]
-
-    def spread(part, grad):
-        keep(part, grad)
-        for k in (4, 2, 6, 0):
+        for k in (2, 1, 3, 0):
             for axis in range(2):
-                own, device, _, _ = along[axis]
-                grad_send(axis, part, k, own, partner if k == 0 else device((own + k) % group))
-
-    def forward(part, k):
-        for axis in range(2):
-            src = (along[axis][0] + group - k) % group
-            grad_copy(axis, part, k, src, me).wait_recv()
-            grad_send(axis, part, k + 1, src, partner)
+                at = pl.ds(pl.multiple_of(items(axis) * slots + part * ql, ql), ql)
+                ref = grads[axis].at[at]
+                if k:
+                    device = gatherer(axis, (chips[axis] + k) % n_mp)
+                    remote(ref, ref, gr_s.at[axis], gr_r.at[k], (device, my)).start()
+                else:
+
+                    @pl.when(core != home[axis])
+                    def _():
+                        remote(ref, ref, gr_s.at[axis], gr_r.at[0], (partner, my)).start()
 
     def share(grad, part, got, send_sem, recv_sem):
         for k in (2, 1, 3):
@@ -439,51 +431,42 @@
     spread(1, grad_d)
     phase("share_d")
     own_d = share(grad_d, part_d, got_d, pd_s, pd_r)
-    phase("forward_q")
-    for k in (2, 6, 4):
-        forward(0, k)
+    phase("rt_wait")
     await_got(rt_others, rt_r)
-    chips = (z, x)
-    total_h = [None, None]
-
-    def chip_product(axis, k):
-        at = pl.ds(pl.multiple_of((chips[axis] + 4 - k // 2) % 4 * 2 * slots, slots), 2 * slots)
-        term = jnp.dot(
-            rt_buf[axis, :, :, at].reshape(n_mp * hrows, 2 * slots), grads[axis][at, :],
-            preferred_element_type=F32,
-        )
-        return term if total_h[axis] is None else total_h[axis] + term
-
-    def chip_arrived(k):
-        await_got(rows.at[0], gp_r.at[(k + 1) // 2 if k else 0])
-
-    phase("own_h")
-    chip_arrived(0)
+    phase(None)
+
+    def head_part(axis):
+        def arrived(k):
+            await_got(grads[axis].at[pl.ds(0, (4 if k else 2) * ql)], gr_r.at[k])
+            pos = (chips[axis] + n_mp - k) % n_mp
+            at = pl.ds(pl.multiple_of(pos * 2 * slots, 2 * slots), 2 * slots)
+            return jnp.dot(
+                rt_buf[:, :, :, at].reshape(8 * hrows, 2 * slots), grads[axis][at, :],
+                preferred_element_type=F32,
+            )
+
+        total = None
+        for k in (0, 1, 3, 2):
+            with jax.named_scope("chip_h"):
+                term = arrived(k)
+                total = term if total is None else total + term
+        with jax.named_scope("head"):
+            full_h[axis][...] = total.reshape(8, hrows, -1)
+            part_h[axis][...] = full_h[axis][...].astype(BF16)
+            for k in (2, 1, 3):
+                pos = (spots[axis] + k) % n_mp
+                for c in range(2):
+                    remote(
+                        part_h[axis].at[pos * 2 + c], got_h[axis].at[k],
+                        hg_s.at[axis], hg_r.at[axis], (reducer(axis, pos, c), my),
+                    ).start()
+            remote(
+                part_h[axis].at[spots[axis] * 2 + 1 - home[axis]], got_h[axis].at[0],
+                hg_s.at[axis], hg_r.at[axis], (partner, my),
+            ).start()
+
     for axis in range(2):
-        total_h[axis] = chip_product(axis, 0)
-    phase("forward_d")
-    for k in (2, 6, 4):
-        forward(1, k)
-    for k in (2, 6):
-        phase("near_h")
-        chip_arrived(k)
-        for axis in range(2):
-            total_h[axis] = chip_product(axis, k)
-    phase("settle")
-    chip_arrived(4)
-    phase("head")
-    own_h = []
-    for axis in range(2):
-        mine = along[axis][3]
-        full_h[axis][...] = chip_product(axis, 4).reshape(n_mp, hrows, -1)
-        part_h[axis][...] = full_h[axis][...].astype(BF16)
-        for k in (2, 1, 3):
-            peer = (mine + k) % n_mp
-            remote(
-                part_h[axis].at[peer], got_h[axis].at[k], hg_s.at[axis], hg_r.at[axis],
-                (along[axis][2](peer), my),
-            ).start()
-        own_h.append(full_h[axis][mine])
+        pl.when(core == home[axis])(functools.partial(head_part, axis))
     phase("query_out")
     await_got(got_q.at[pl.ds(1, n_mp - 1)], pq_r)
     qg_ref[...] = gather_parts(own_q, got_q).astype(BF16)
@@ -493,8 +476,19 @@
     dg_ref[...] = gather_parts(own_d, got_d).astype(BF16)
     phase("head_out")
     for axis in range(2):
-        await_got(got_h[axis].at[pl.ds(1, n_mp - 1)], hg_r.at[axis])
-        hg_ref[:, cuts[axis] : cuts[axis + 1]] = gather_parts(own_h[axis], got_h[axis])
+        columns = slice(cuts[axis], cuts[axis + 1])
+
+        @pl.when(core == home[axis])
+        def _():
+            await_got(got_h[axis].at[pl.ds(1, n_mp - 1)], hg_r.at[axis])
+            mine = full_h[axis][spots[axis] * 2 + home[axis]]
+            hg_ref[:, columns] = gather_parts(mine, got_h[axis])
+
+        @pl.when(core != home[axis])
+        def _():
+            await_got(got_h[axis], hg_r.at[axis])
+            hg_ref[:, columns] = gather_parts(got_h[axis][0].astype(F32), got_h[axis])
+
     phase("drain")
     await_sent(rows.at[pl.ds(0, 3)], ag_s)
     await_sent(out_buf.at[pl.ds(0, n_dp - 1)], fe_s)
@@ -502,8 +496,16 @@
     await_sent(score_buf.at[pl.ds(0, n_mp - 1)], sc_s)
     await_sent(back_buf.at[pl.ds(0, n_dp - 1)], ba_s)
     for axis in range(2):
-        await_sent(grads[axis].at[pl.ds(0, 896)], gr_s.at[axis])
-        await_sent(part_h[axis].at[pl.ds(1, n_mp - 1)], hg_s.at[axis])
+
+        @pl.when(core == home[axis])
+        def _():
+            await_sent(grads[axis].at[pl.ds(0, 6 * ql)], gr_s.at[axis])
+            await_sent(part_h[axis].at[pl.ds(0, 7)], hg_s.at[axis])
+
+        @pl.when(core != home[axis])
+        def _():
+            await_sent(grads[axis].at[pl.ds(0, 8 * ql)], gr_s.at[axis])
+
     await_sent(part_q.at[pl.ds(1, n_mp - 1)], pq_s)
     await_sent(part_d.at[pl.ds(1, n_mp - 1)], pd_s)
     phase(None)
@@ -545,7 +547,7 @@
             pltpu.VMEM((4, 2 * ql, cols), BF16),
             pltpu.VMEM((4 * cols, cols), BF16),
             pltpu.VMEM((4, 4, 2, 80, 128), BF16),
-            pltpu.VMEM((2, 4, 80, 1024), BF16),
+            pltpu.VMEM((4, 2, 80, 1024), BF16),
             pltpu.VMEM((1024, 384), BF16),
             pltpu.VMEM((1024, 256), BF16),
             pltpu.VMEM((32, 4, cols), BF16),
@@ -557,14 +559,14 @@
             pltpu.VMEM((4, ql, cols), BF16),
             pltpu.VMEM((4, ql, cols), BF16),
             pltpu.VMEM((4, ql, cols), BF16),
-            pltpu.VMEM((4, 80, 384), F32),
-            pltpu.VMEM((4, 80, 256), F32),
-            pltpu.VMEM((4, 80, 384), BF16),
-            pltpu.VMEM((4, 80, 256), BF16),
+            pltpu.VMEM((8, 80, 384), F32),
+            pltpu.VMEM((8, 80, 256), F32),
+            pltpu.VMEM((8, 80, 384), BF16),
+            pltpu.VMEM((8, 80, 256), BF16),
             pltpu.VMEM((4, 80, 384), BF16),
             pltpu.VMEM((4, 80, 256), BF16),
             dma((10,)), one, dma((14,)), one, one, one, one, one, one, one, one,
-            dma((2,)), dma((2, 2, 3)), dma((4,)), one, one, one, one, dma((2,)), dma((2,)),
+            dma((2,)), dma((4,)), one, one, one, one, dma((2,)), dma((2,)),
             pltpu.SemaphoreType.REGULAR((4,)),
         ],
         compiler_params=pltpu.CompilerParams(

time: 45 us -> 44 us (0.978)
  Pallas kernels: 44.3 us -> 43.3 us
    pallas_call x1, Pallas kernels: 43.5 us -> 42.5 us  [on_device(): pl.pallas_call(kernel, out_shape=shapes, in_specs=[hbm] * 7, out_specs=(v...]
where the time goes in v5:
time: 44 us; the launch traced here: 43.9 us
  Pallas kernels  43.3 us (98%)
  between operations  0.64 us (1%)
    pallas_call x1, Pallas kernels, on_device(): pl.pallas_call(kernel, out_shape=shapes, in_specs=[hbm] * 7, out_specs=(v...  42.5 us

profile of v5, /device:TPU:1, one launch (start us, length us, event | category | flops | bytes accessed | tf_op | source)
XLA Modules:
  0.0 43.9 jit_solution(17738245593050551286)
XLA Ops:
  0.6 42.5 %shard_map.94 = (bf16[64,640]{1,0:T(8,128)(2,1)S(1)}, bf16[64,640]{1,0:T(8,128)(2,1)S(1)}, f32[80,640]{1,0:T(8,128)S(1)}) custom-call(f32[7]{0:T(128)} %scale_hbm.1, f32[7,64]{1,0:T(8,128)} %bitcast.1, s32[64,128]{1,0:T(8,128)} %short_hbm.1, s32[1,128]{1,0:T(1,128)} %send_hbm.1, bf16[64,640]{1,0:T(8,128)(2,1)} %q_hbm.1, bf16[64,640]{1,0:T(8,128)(2,1)} %d_hbm.1, ...), custom_call_target="tpu_custom_call" | custom-call | tf_op jit(solution)/shard_map/pallas_call | solution.py:537
  43.1 0.8 %shard_map.95 = (bf16[64,640]{1,0:T(8,128)(2,1)}, bf16[64,640]{1,0:T(8,128)(2,1)}, f32[80,640]{1,0:T(8,128)}) custom-call(bf16[64,640]{1,0:T(8,128)(2,1)S(1)} %get-tuple-element.6.a, bf16[64,640]{1,0:T(8,128)(2,1)S(1)} %get-tuple-element.7.b, f32[80,640]{1,0:T(8,128)S(1)} %get-tuple-element.8.c), custom_call_target="tpu_custom_call" | custom-call | tf_op jit(solution)/shard_map/pallas_call | solution.py:577

commit v6 on v5

--- a/solution.py
+++ b/solution.py
@@ -147,42 +147,45 @@
     pl.semaphore_wait(barrier, len(near))
 
     half, quarter = ql // 2, ql // 4
+    row_pieces = (
+        (0, half, far),
+        (half, quarter, right),
+        (half + quarter, quarter, right),
+        (0, half, right),
+        (half + quarter, quarter, left),
+        (0, half + quarter, left),
+        (half, quarter, right),
+        (half + quarter, quarter, left),
+    )
 
     def row_copy(part, slot, src):
-        first, count, peer = (
-            (0, half, far),
-            (0, ql, right),
-            (half, quarter, left),
-            (half + quarter, quarter, left),
-            (0, half, left),
-            (half, quarter, left),
-            (half + quarter, quarter, left),
-        )[slot]
+        first, count, peer = row_pieces[slot]
         at = pl.ds((1 - part) * ql + first, count)
-        slot = part * 7 + slot
+        slot = part * 8 + slot
         return remote(
             rows.at[src, at], rows.at[src, at], ag_s, ag_r.at[slot], (me, peer)
         )
 
     def rows_start(part):
-        for slot in (0, 2, 1, 3, 4):
+        for slot in (1, 4, 0, 2, 3, 5):
             row_copy(part, slot, my).start()
 
     def rows_relay(part):
+        for slot, src in ((1, left), (4, right)):
+            row_copy(part, slot, src).wait_recv()
+            row_copy(part, 6 if slot == 1 else 7, src).start()
+
+    def rows_right(part):
+        row_copy(part, 5, right).wait_recv()
+        return product_of(part, right)
+
+    def rows_left(part):
         for slot in (2, 3):
-            row_copy(part, slot, right).wait_recv()
-            row_copy(part, slot + 3, right).start()
-
-    def rows_right(part):
-        row_copy(part, 4, right).wait_recv()
-        return product_of(part, right)
-
-    def rows_left(part):
-        row_copy(part, 1, left).wait_recv()
+            row_copy(part, slot, left).wait_recv()
         return product_of(part, left)
 
     def rows_far(part):
-        for slot in (0, 5, 6):
+        for slot in (0, 6, 7):
             row_copy(part, slot, far).wait_recv()
         return product_of(part, far)
 
@@ -196,14 +199,16 @@
     chips = (z, x)
     spots = (x, z)
 
+    bands = (((0, 384),), ((0, 256),))
+
     def gatherer(axis, pos):
         return x * group + pos * 2 + home[0] if axis == 0 else pos * group + z * 2 + home[1]
 
     def reducer(axis, pos, c):
         return pos * group + z * 2 + c if axis == 0 else x * group + pos * 2 + c
 
-    def items(axis):
-        return chips[axis] * 2 + core
+    def place(k):
+        return pl.multiple_of(k * 2 * slots + core * slots, slots)
 
     def turned(axis, pos):
         return rows_t.at[:, pos] if axis == 0 else rows_t.at[pos]
@@ -214,22 +219,22 @@
 
     def turn_start(axes):
         for axis in axes:
-            at = pl.ds(pl.multiple_of(items(axis) * slots, slots), slots)
+            own = pl.ds(place(0), slots)
             for k in (2, 1, 3):
                 pos = (chips[axis] + k) % n_mp
                 remote(
-                    turned(axis, pos), rt_buf.at[:, :, :, at], rt_s, rt_r,
+                    turned(axis, pos), rt_buf.at[:, :, :, pl.ds(place(k), slots)], rt_s, rt_r,
                     (gatherer(axis, pos), my),
                 ).start()
 
             @pl.when(core == home[axis])
             def _():
-                rt_buf[:, :, :, at] = turned(axis, chips[axis])[...]
+                rt_buf[:, :, :, own] = turned(axis, chips[axis])[...]
 
             @pl.when(core != home[axis])
             def _():
                 remote(
-                    turned(axis, chips[axis]), rt_buf.at[:, :, :, at], rt_s, rt_r, (partner, my)
+                    turned(axis, chips[axis]), rt_buf.at[:, :, :, own], rt_s, rt_r, (partner, my)
                 ).start()
 
     rt_others = rt_buf.at[:, :, :, pl.ds(0, (group - 1) * slots)]
@@ -293,7 +298,7 @@
 
     phase("turn0")
     turn_rows()
-    turn_start((0,))
+    turn_start((1, 0))
     phase("mask")
     col = lax.broadcasted_iota(jnp.int32, (1, cols), 1)
     seg_col = [
@@ -308,24 +313,18 @@
         for s in range(LOCAL)
     ]
 
-    phase("fetch_wait")
-    await_got(fetched.at[pl.ds(0, n_dp - 1)], fe_r)
-    phase("turn")
-    turn_start((1,))
-    phase("score")
-    docs = fetched[...].reshape(slots, cols)
-    pieces = contract(q_seg, docs, 1, 1)
-    scores = []
-    for s in range(LOCAL):
-        piece = pieces[s * ql : (s + 1) * ql]
-        scores.append(piece if s == 0 else scores[-1] + piece)
-
     diag = lax.broadcasted_iota(jnp.int32, (ql, slots), 0) == lane
     pos_row = jnp.sum(
         jnp.where(diag, jnp.broadcast_to(pos_prefix[-1], (ql, slots)), 0.0), axis=0, keepdims=True
     )
-    score_buf[my, 0:ql, :] = scores[-1]
     score_buf[my, ql : ql + 8, :] = jnp.broadcast_to(pos_row, (8, slots))
+
+    phase("fetch_wait")
+    await_got(fetched.at[pl.ds(0, n_dp - 1)], fe_r)
+    phase("score")
+    docs = fetched[...].reshape(slots, cols)
+    whole = contract(qp, docs, 1, 1)
+    score_buf[my, 0:ql, :] = whole
     for peer in (far, right, left):
         remote(score_buf.at[my], score_buf.at[my], sc_s, sc_r, (me, peer)).start()
 
@@ -334,7 +333,16 @@
         scale = scale_ref[w] * (1.0 / math.sqrt(bounds[w + 1]))
         return softmax_terms(score, pos, count, scale, weight[:, w : w + 1])
 
+    pieces = contract(q_seg[: 4 * ql], docs, 1, 1)
+    scores = []
+    for s in range(LOCAL - 1):
+        piece = pieces[s * ql : (s + 1) * ql]
+        scores.append(piece if s == 0 else scores[-1] + piece)
+    scores.append(whole)
     narrow = [width(w, scores[w], pos_prefix[w]) for w in range(LOCAL)]
+    for s in reversed(range(LOCAL - 1)):
+        narrow[s] = tuple(a + b for a, b in zip(narrow[s], narrow[s + 1]))
+    narrow = [tuple(jnp.where(my == 0, a, 0.0) for a in terms) for terms in narrow]
     doc_seg = [docs * m.astype(BF16) for m in seg_col]
     wide_at = 256
     docs_low = jnp.concatenate([m[:, :wide_at] for m in doc_seg[:4]], axis=0)
@@ -344,26 +352,20 @@
     await_got(score_buf.at[pl.ds(0, n_mp - 1)], sc_r)
     phase("wide")
     parts = [score_buf[m, 0:ql, :] for m in range(n_mp)]
-    pos_parts = [
+    pos_rows = [score_buf[m, ql : ql + 8, :] for m in range(n_mp)]
+    pos_row5 = pos_rows[0] + pos_rows[1]
+    pos5, pos6 = [
         jnp.sum(
-            jnp.where(diag, jnp.concatenate([score_buf[m, ql : ql + 8, :]] * 8, axis=0), 0.0),
-            axis=1,
-            keepdims=True,
+            jnp.where(diag, jnp.concatenate([row] * 8, axis=0), 0.0), axis=1, keepdims=True
         )
-        for m in range(n_mp)
+        for row in (pos_row5, pos_row5 + (pos_rows[2] + pos_rows[3]))
     ]
-    score5, pos5 = parts[0] + parts[1], pos_parts[0] + pos_parts[1]
+    score5 = parts[0] + parts[1]
     neg5, posg5 = width(5, score5, pos5)
-    neg6, posg6 = width(6, score5 + (parts[2] + parts[3]), pos5 + (pos_parts[2] + pos_parts[3]))
+    neg6, posg6 = width(6, score5 + (parts[2] + parts[3]), pos6)
     run_neg = neg6 + jnp.where(my <= 1, neg5, 0.0)
     run_pos = posg6 + jnp.where(my <= 1, posg5, 0.0)
-    coeff = [None] * LOCAL
-    pos_cols = jnp.zeros((ql, cols), F32)
-    for s in reversed(range(LOCAL)):
-        run_neg = run_neg + jnp.where(my == 0, narrow[s][0], 0.0)
-        run_pos = run_pos + jnp.where(my == 0, narrow[s][1], 0.0)
-        coeff[s] = run_neg.astype(BF16)
-        pos_cols = pos_cols + run_pos * seg_col[s]
+    coeff = [(run_neg + narrow[s][0]).astype(BF16) for s in range(LOCAL)]
 
     phase("by_slot")
     by_slot = jnp.concatenate(
@@ -380,6 +382,9 @@
     returned[me] = back_buf[me]
 
     phase("grad_q")
+    pos_cols = (run_pos + narrow[0][1]) * seg_col[0]
+    for s in range(1, LOCAL):
+        pos_cols = pos_cols + (run_pos + narrow[s][1]) * seg_col[s]
     query_back = jnp.concatenate(
         [
             jnp.dot(jnp.concatenate(coeff[:4], axis=1), docs_low, preferred_element_type=F32),
@@ -391,20 +396,23 @@
 
     def spread(part, grad):
         for axis in range(2):
-            at = pl.ds(pl.multiple_of(items(axis) * slots + part * ql, ql), ql)
+            at = pl.ds(pl.multiple_of(place(0) + part * ql, ql), ql)
             grads[axis][at, :] = grad[:, cuts[axis] : cuts[axis + 1]]
-        for k in (2, 1, 3, 0):
-            for axis in range(2):
-                at = pl.ds(pl.multiple_of(items(axis) * slots + part * ql, ql), ql)
-                ref = grads[axis].at[at]
-                if k:
-                    device = gatherer(axis, (chips[axis] + k) % n_mp)
-                    remote(ref, ref, gr_s.at[axis], gr_r.at[k], (device, my)).start()
-                else:
-
-                    @pl.when(core != home[axis])
-                    def _():
-                        remote(ref, ref, gr_s.at[axis], gr_r.at[0], (partner, my)).start()
+        for band in range(len(bands[0])):
+            for k in (2, 1, 3, 0):
+                for axis in range(2):
+                    columns = slice(*bands[axis][band])
+                    own = pl.ds(pl.multiple_of(place(0) + part * ql, ql), ql)
+                    there = pl.ds(pl.multiple_of(place(k) + part * ql, ql), ql)
+                    src, dst = grads[axis].at[own, columns], grads[axis].at[there, columns]
+                    if k:
+                        device = gatherer(axis, (chips[axis] + k) % n_mp)
+                        remote(src, dst, gr_s.at[axis], gr_r, (device, my)).start()
+                    else:
+
+                        @pl.when(core != home[axis])
+                        def _():
+                            remote(src, dst, gr_s.at[axis], gr_r, (partner, my)).start()
 
     def share(grad, part, got, send_sem, recv_sem):
         for k in (2, 1, 3):
@@ -436,34 +444,27 @@
     phase(None)
 
     def head_part(axis):
-        def arrived(k):
-            await_got(grads[axis].at[pl.ds(0, (4 if k else 2) * ql)], gr_r.at[k])
-            pos = (chips[axis] + n_mp - k) % n_mp
-            at = pl.ds(pl.multiple_of(pos * 2 * slots, 2 * slots), 2 * slots)
-            return jnp.dot(
-                rt_buf[:, :, :, at].reshape(8 * hrows, 2 * slots), grads[axis][at, :],
-                preferred_element_type=F32,
-            )
-
-        total = None
-        for k in (0, 1, 3, 2):
-            with jax.named_scope("chip_h"):
-                term = arrived(k)
-                total = term if total is None else total + term
-        with jax.named_scope("head"):
-            full_h[axis][...] = total.reshape(8, hrows, -1)
-            part_h[axis][...] = full_h[axis][...].astype(BF16)
-            for k in (2, 1, 3):
-                pos = (spots[axis] + k) % n_mp
-                for c in range(2):
+        with jax.named_scope("gather_h"):
+            await_got(grads[axis].at[pl.ds(0, 7 * slots)], gr_r)
+        for n in (2, 1, 3, 0):
+            pos = (spots[axis] + n) % n_mp
+            with jax.named_scope("head%d" % n):
+                block = jnp.dot(
+                    rt_buf[pos].reshape(2 * hrows, n_mp * 2 * slots), grads[axis][...],
+                    preferred_element_type=F32,
+                )
+                part_h[axis][pl.ds(pos * 2, 2)] = block.astype(BF16).reshape(2, hrows, -1)
+                if n == 0:
+                    full_h[axis][...] = block[home[axis] * hrows : (home[axis] + 1) * hrows]
                     remote(
-                        part_h[axis].at[pos * 2 + c], got_h[axis].at[k],
-                        hg_s.at[axis], hg_r.at[axis], (reducer(axis, pos, c), my),
+                        part_h[axis].at[pos * 2 + 1 - home[axis]], got_h[axis].at[0],
+                        hg_s.at[axis], hg_r.at[axis], (partner, my),
                     ).start()
-            remote(
-                part_h[axis].at[spots[axis] * 2 + 1 - home[axis]], got_h[axis].at[0],
-                hg_s.at[axis], hg_r.at[axis], (partner, my),
-            ).start()
+                for i in range(2 if n else 0):
+                    remote(
+                        part_h[axis].at[pos * 2 + i], got_h[axis].at[n],
+                        hg_s.at[axis], hg_r.at[axis], (reducer(axis, pos, i), my),
+                    ).start()
 
     for axis in range(2):
         pl.when(core == home[axis])(functools.partial(head_part, axis))
@@ -481,8 +482,7 @@
         @pl.when(core == home[axis])
         def _():
             await_got(got_h[axis].at[pl.ds(1, n_mp - 1)], hg_r.at[axis])
-            mine = full_h[axis][spots[axis] * 2 + home[axis]]
-            hg_ref[:, columns] = gather_parts(mine, got_h[axis])
+            hg_ref[:, columns] = gather_parts(full_h[axis][...], got_h[axis])
 
         @pl.when(core != home[axis])
         def _():
@@ -559,14 +559,14 @@
             pltpu.VMEM((4, ql, cols), BF16),
             pltpu.VMEM((4, ql, cols), BF16),
             pltpu.VMEM((4, ql, cols), BF16),
-            pltpu.VMEM((8, 80, 384), F32),
-            pltpu.VMEM((8, 80, 256), F32),
+            pltpu.VMEM((80, 384), F32),
+            pltpu.VMEM((80, 256), F32),
             pltpu.VMEM((8, 80, 384), BF16),
             pltpu.VMEM((8, 80, 256), BF16),
             pltpu.VMEM((4, 80, 384), BF16),
             pltpu.VMEM((4, 80, 256), BF16),
-            dma((10,)), one, dma((14,)), one, one, one, one, one, one, one, one,
-            dma((2,)), dma((4,)), one, one, one, one, dma((2,)), dma((2,)),
+            dma((10,)), one, dma((16,)), one, one, one, one, one, one, one, one,
+            dma((2,)), one, one, one, one, one, dma((2,)), dma((2,)),
             pltpu.SemaphoreType.REGULAR((4,)),
         ],
         compiler_params=pltpu.CompilerParams(

time: 44 us -> 42.2 us (0.959)
  Pallas kernels: 43.3 us -> 41.4 us
    pallas_call x1, Pallas kernels: 42.5 us -> 40.7 us  [on_device(): pl.pallas_call(kernel, out_shape=shapes, in_specs=[hbm] * 7, out_specs=(v...]
where the time goes in v6:
time: 42.2 us; the launch traced here: 42.1 us
  Pallas kernels  41.4 us (98%)
  between operations  0.64 us (2%)
    pallas_call x1, Pallas kernels, on_device(): pl.pallas_call(kernel, out_shape=shapes, in_specs=[hbm] * 7, out_specs=(v...  40.7 us

profile of v6, /device:TPU:1, one launch (start us, length us, event | category | flops | bytes accessed | tf_op | source)
XLA Modules:
  0.0 42.1 jit_solution(1888943320466935824)
XLA Ops:
  0.6 40.7 %shard_map.94 = (bf16[64,640]{1,0:T(8,128)(2,1)S(1)}, bf16[64,640]{1,0:T(8,128)(2,1)S(1)}, f32[80,640]{1,0:T(8,128)S(1)}) custom-call(f32[7]{0:T(128)} %scale_hbm.1, f32[7,64]{1,0:T(8,128)} %bitcast.1, s32[64,128]{1,0:T(8,128)} %short_hbm.1, s32[1,128]{1,0:T(1,128)} %send_hbm.1, bf16[64,640]{1,0:T(8,128)(2,1)} %q_hbm.1, bf16[64,640]{1,0:T(8,128)(2,1)} %d_hbm.1, ...), custom_call_target="tpu_custom_call" | custom-call | tf_op jit(solution)/shard_map/pallas_call | solution.py:537
  41.3 0.8 %shard_map.95 = (bf16[64,640]{1,0:T(8,128)(2,1)}, bf16[64,640]{1,0:T(8,128)(2,1)}, f32[80,640]{1,0:T(8,128)}) custom-call(bf16[64,640]{1,0:T(8,128)(2,1)S(1)} %get-tuple-element.6.a, bf16[64,640]{1,0:T(8,128)(2,1)S(1)} %get-tuple-element.7.b, f32[80,640]{1,0:T(8,128)S(1)} %get-tuple-element.8.c), custom_call_target="tpu_custom_call" | custom-call | tf_op jit(solution)/shard_map/pallas_call | solution.py:577

commit v7 on v6

--- a/solution.py
+++ b/solution.py
@@ -213,9 +213,8 @@
     def turned(axis, pos):
         return rows_t.at[:, pos] if axis == 0 else rows_t.at[pos]
 
-    def turn_rows():
-        for m in range(n_mp):
-            rows_t[m] = rows[m].T.reshape(n_mp, 2, hrows, slots)
+    def turn_rows(m):
+        rows_t[m] = rows[m].T.reshape(n_mp, 2, hrows, slots)
 
     def turn_start(axes):
         for axis in axes:
@@ -255,12 +254,12 @@
     tell(1, z_near)
     phase("relay_d")
     rows_relay(0)
-    load_q.wait()
-    rows_start(1)
     hear(1, 2)
     tell(2, z_near)
     phase("right_d")
     acc = acc + rows_right(0)
+    load_q.wait()
+    rows_start(1)
     hear(2, 2)
     tell(3, (partner,))
     phase("left_d")
@@ -293,29 +292,28 @@
     for k in range(slots):
         count = count + jnp.where((short if k == 0 else pltpu.roll(short, k, 1)) == lane, 1.0, 0.0)
     phase("rows_q")
-    acc = product_of(1, my) + rows_right(1) + rows_left(1) + rows_far(1)
+    acc = product_of(1, my)
+    turn_rows(my)
+    acc = acc + rows_right(1)
+    turn_rows(right)
+    acc = acc + rows_left(1)
+    turn_rows(left)
+    acc = acc + rows_far(1)
     qp = acc.astype(BF16)
 
     phase("turn0")
-    turn_rows()
+    turn_rows(far)
     turn_start((1, 0))
     phase("mask")
     col = lax.broadcasted_iota(jnp.int32, (1, cols), 1)
     seg_col = [
         jnp.where((col >= bounds[s]) & (col < bounds[s + 1]), 1.0, 0.0) for s in range(LOCAL)
     ]
-    q_seg = jnp.concatenate([qp * m.astype(BF16) for m in seg_col], axis=0)
     product = qp.astype(F32) * dp.astype(F32)
-    pos_prefix = [
-        jnp.sum(
-            product * jnp.where(col < bounds[s + 1], 1.0, 0.0), axis=1, keepdims=True
-        )
-        for s in range(LOCAL)
-    ]
-
+    pos_whole = jnp.sum(product, axis=1, keepdims=True)
     diag = lax.broadcasted_iota(jnp.int32, (ql, slots), 0) == lane
     pos_row = jnp.sum(
-        jnp.where(diag, jnp.broadcast_to(pos_prefix[-1], (ql, slots)), 0.0), axis=0, keepdims=True
+        jnp.where(diag, jnp.broadcast_to(pos_whole, (ql, slots)), 0.0), axis=0, keepdims=True
     )
     score_buf[my, ql : ql + 8, :] = jnp.broadcast_to(pos_row, (8, slots))
 
@@ -333,6 +331,13 @@
         scale = scale_ref[w] * (1.0 / math.sqrt(bounds[w + 1]))
         return softmax_terms(score, pos, count, scale, weight[:, w : w + 1])
 
+    q_seg = jnp.concatenate([qp * m.astype(BF16) for m in seg_col], axis=0)
+    pos_prefix = [
+        jnp.sum(
+            product * jnp.where(col < bounds[s + 1], 1.0, 0.0), axis=1, keepdims=True
+        )
+        for s in range(LOCAL - 1)
+    ] + [pos_whole]
     pieces = contract(q_seg[: 4 * ql], docs, 1, 1)
     scores = []
     for s in range(LOCAL - 1):

time: 42.2 us -> 41.8 us (level)
  no operation moved by 1% of the time
where the time goes in v7:
time: 41.8 us; the launch traced here: 41.7 us
  Pallas kernels  41 us (98%)
  between operations  0.64 us (2%)
    pallas_call x1, Pallas kernels, on_device(): pl.pallas_call(kernel, out_shape=shapes, in_specs=[hbm] * 7, out_specs=(v...  40.3 us

profile of v7, /device:TPU:1, one launch (start us, length us, event | category | flops | bytes accessed | tf_op | source)
XLA Modules:
  0.0 41.7 jit_solution(12144239228851003242)
XLA Ops:
  0.6 40.3 %shard_map.94 = (bf16[64,640]{1,0:T(8,128)(2,1)S(1)}, bf16[64,640]{1,0:T(8,128)(2,1)S(1)}, f32[80,640]{1,0:T(8,128)S(1)}) custom-call(f32[7]{0:T(128)} %scale_hbm.1, f32[7,64]{1,0:T(8,128)} %bitcast.1, s32[64,128]{1,0:T(8,128)} %short_hbm.1, s32[1,128]{1,0:T(1,128)} %send_hbm.1, bf16[64,640]{1,0:T(8,128)(2,1)} %q_hbm.1, bf16[64,640]{1,0:T(8,128)(2,1)} %d_hbm.1, ...), custom_call_target="tpu_custom_call" | custom-call | tf_op jit(solution)/shard_map/pallas_call | solution.py:542
  40.9 0.8 %shard_map.95 = (bf16[64,640]{1,0:T(8,128)(2,1)}, bf16[64,640]{1,0:T(8,128)(2,1)}, f32[80,640]{1,0:T(8,128)}) custom-call(bf16[64,640]{1,0:T(8,128)(2,1)S(1)} %get-tuple-element.6.a, bf16[64,640]{1,0:T(8,128)(2,1)S(1)} %get-tuple-element.7.b, f32[80,640]{1,0:T(8,128)S(1)} %get-tuple-element.8.c), custom_call_target="tpu_custom_call" | custom-call | tf_op jit(solution)/shard_map/pallas_call | solution.py:582

commit v8 on v7

--- a/solution.py
+++ b/solution.py
@@ -59,7 +59,7 @@
     scale_ref, loss_ref, short_ref, send_ref, rows, head, rows_t, rt_buf, grads_0, grads_1,
     out_buf, fetched, back_buf, returned,
     score_buf, part_q, got_q, part_d, got_d,
-    full_0, full_1, part_0, part_1, got_0, got_1,
+    own_0, own_1, full_0, full_1, part_0, part_1, got_0, got_1,
     load_sem, ag_s, ag_r, fe_s, fe_r, sc_s, sc_r, rt_s, rt_r, ba_s, ba_r,
     gr_s, gr_r, pq_s, pq_r, pd_s, pd_r, hg_s, hg_r, word,
 ):
@@ -69,8 +69,8 @@
     block = 4
     hrows = 80
     cuts = (0, 384, cols)
-    grads, full_h, part_h, got_h = (
-        (grads_0, grads_1), (full_0, full_1), (part_0, part_1), (got_0, got_1)
+    grads, own_h, full_h, part_h, got_h = (
+        (grads_0, grads_1), (own_0, own_1), (full_0, full_1), (part_0, part_1), (got_0, got_1)
     )
     me = lax.axis_index("dp")
     my = lax.axis_index("mp")
@@ -161,7 +161,7 @@
     def row_copy(part, slot, src):
         first, count, peer = row_pieces[slot]
         at = pl.ds((1 - part) * ql + first, count)
-        slot = part * 8 + slot
+        slot = part * 5 + (0, 1, 2, 2, 3, 4, 0, 0)[slot]
         return remote(
             rows.at[src, at], rows.at[src, at], ag_s, ag_r.at[slot], (me, peer)
         )
@@ -180,13 +180,11 @@
         return product_of(part, right)
 
     def rows_left(part):
-        for slot in (2, 3):
-            row_copy(part, slot, left).wait_recv()
+        await_got(rows.at[left, pl.ds(0, half + quarter)], ag_r.at[part * 5 + 2])
         return product_of(part, left)
 
     def rows_far(part):
-        for slot in (0, 6, 7):
-            row_copy(part, slot, far).wait_recv()
+        await_got(rows.at[far, pl.ds(0, ql)], ag_r.at[part * 5])
         return product_of(part, far)
 
     def product_of(part, src):
@@ -412,12 +410,12 @@
                     src, dst = grads[axis].at[own, columns], grads[axis].at[there, columns]
                     if k:
                         device = gatherer(axis, (chips[axis] + k) % n_mp)
-                        remote(src, dst, gr_s.at[axis], gr_r, (device, my)).start()
+                        remote(src, dst, gr_s.at[axis], gr_r.at[1], (device, my)).start()
                     else:
 
                         @pl.when(core != home[axis])
                         def _():
-                            remote(src, dst, gr_s.at[axis], gr_r, (partner, my)).start()
+                            remote(src, dst, gr_s.at[axis], gr_r.at[0], (partner, my)).start()
 
     def share(grad, part, got, send_sem, recv_sem):
         for k in (2, 1, 3):
@@ -450,12 +448,18 @@
 
     def head_part(axis):
         with jax.named_scope("gather_h"):
-            await_got(grads[axis].at[pl.ds(0, 7 * slots)], gr_r)
+            chip = 2 * slots
+            await_got(grads[axis].at[pl.ds(0, slots)], gr_r.at[0])
+            own_h[axis][...] = jnp.dot(
+                rt_buf[:, :, :, :chip].reshape(n_mp * 2 * hrows, chip), grads[axis][:chip],
+                preferred_element_type=F32,
+            ).reshape(n_mp, 2 * hrows, -1)
+            await_got(grads[axis].at[pl.ds(0, 6 * slots)], gr_r.at[1])
         for n in (2, 1, 3, 0):
             pos = (spots[axis] + n) % n_mp
             with jax.named_scope("head%d" % n):
-                block = jnp.dot(
-                    rt_buf[pos].reshape(2 * hrows, n_mp * 2 * slots), grads[axis][...],
+                block = own_h[axis][pos] + jnp.dot(
+                    rt_buf[pos, :, :, chip:].reshape(2 * hrows, 3 * chip), grads[axis][chip:],
                     preferred_element_type=F32,
                 )
                 part_h[axis][pl.ds(pos * 2, 2)] = block.astype(BF16).reshape(2, hrows, -1)
@@ -564,14 +568,16 @@
             pltpu.VMEM((4, ql, cols), BF16),
             pltpu.VMEM((4, ql, cols), BF16),
             pltpu.VMEM((4, ql, cols), BF16),
+            pltpu.VMEM((4, 160, 384), F32),
+            pltpu.VMEM((4, 160, 256), F32),
             pltpu.VMEM((80, 384), F32),
             pltpu.VMEM((80, 256), F32),
             pltpu.VMEM((8, 80, 384), BF16),
             pltpu.VMEM((8, 80, 256), BF16),
             pltpu.VMEM((4, 80, 384), BF16),
             pltpu.VMEM((4, 80, 256), BF16),
-            dma((10,)), one, dma((16,)), one, one, one, one, one, one, one, one,
-            dma((2,)), one, one, one, one, one, dma((2,)), dma((2,)),
+            dma((10,)), one, dma((10,)), one, one, one, one, one, one, one, one,
+            dma((2,)), dma((2,)), one, one, one, one, dma((2,)), dma((2,)),
             pltpu.SemaphoreType.REGULAR((4,)),
         ],
         compiler_params=pltpu.CompilerParams(

time: 41.8 us -> 41.7 us (level)
  no operation moved by 1% of the time
where the time goes in v8:
time: 41.7 us; the launch traced here: 41.6 us
  Pallas kernels  40.9 us (98%)
  between operations  0.64 us (2%)
    pallas_call x1, Pallas kernels, on_device(): pl.pallas_call(kernel, out_shape=shapes, in_specs=[hbm] * 7, out_specs=(v...  40.2 us

profile of v8, /device:TPU:1, one launch (start us, length us, event | category | flops | bytes accessed | tf_op | source)
XLA Modules:
  0.0 41.6 jit_solution(16799583625823539439)
XLA Ops:
  0.6 40.2 %shard_map.94 = (bf16[64,640]{1,0:T(8,128)(2,1)S(1)}, bf16[64,640]{1,0:T(8,128)(2,1)S(1)}, f32[80,640]{1,0:T(8,128)S(1)}) custom-call(f32[7]{0:T(128)} %scale_hbm.1, f32[7,64]{1,0:T(8,128)} %bitcast.1, s32[64,128]{1,0:T(8,128)} %short_hbm.1, s32[1,128]{1,0:T(1,128)} %send_hbm.1, bf16[64,640]{1,0:T(8,128)(2,1)} %q_hbm.1, bf16[64,640]{1,0:T(8,128)(2,1)} %d_hbm.1, ...), custom_call_target="tpu_custom_call" | custom-call | tf_op jit(solution)/shard_map/pallas_call | solution.py:546
  40.8 0.8 %shard_map.95 = (bf16[64,640]{1,0:T(8,128)(2,1)}, bf16[64,640]{1,0:T(8,128)(2,1)}, f32[80,640]{1,0:T(8,128)}) custom-call(bf16[64,640]{1,0:T(8,128)(2,1)S(1)} %get-tuple-element.6.a, bf16[64,640]{1,0:T(8,128)(2,1)S(1)} %get-tuple-element.7.b, f32[80,640]{1,0:T(8,128)S(1)} %get-tuple-element.8.c), custom_call_target="tpu_custom_call" | custom-call | tf_op jit(solution)/shard_map/pallas_call | solution.py:588
